TPU v7x, 32 devices: a whole 2x2x4 slice. The times are simulated.
32 devices in a mesh: dp: 8 (over y, x, core), tm: 4 (over z).
Axes of the slice: x: 2, y: 2, z: 4, core: 2. Of those that a mesh axis runs over, the one named last changes fastest.
Arguments:
- audio: float32 [24, 8, 1024], P('dp', None, 'tm'), may hold values from -3.15 to 3.15, as said below
- mel_frames: bfloat16 [24, 1024, 640], P('dp', 'tm'), may hold values from -6 to 6
- start_weight: float32 [4, 512], replicated, may hold values from -3 to 3
- input_weight: bfloat16 [2, 3, 512, 1024], replicated, may hold values from -0.15625 to 0.15625
- cond_weight: bfloat16 [2, 640, 1024], replicated, may hold values from -0.25 to 0.25
- res_weight: bfloat16 [1, 512, 1024], replicated, may hold values from -0.25 to 0.25
- last_weight: bfloat16 [512, 512], replicated, may hold values from -0.25 to 0.25
- end_weight: bfloat16 [512, 8], replicated, may hold values from -0.25 to 0.25
Outputs:
- latent: float32 [24, 4, 1024], P('dp', None, 'tm')
- audio_grad: float32 [24, 8, 1024], P('dp', None, 'tm')
- batch_loss: float32 [], replicated
- input_weight_grad: float32 [2, 3, 512, 1024], P(None, None, 'dp', 'tm')
- cond_weight_grad: float32 [2, 640, 1024], P(None, 'dp', 'tm')
- res_weight_grad: float32 [1, 512, 1024], P(None, 'dp', 'tm')
- last_weight_grad: float32 [512, 512], replicated
- end_weight_grad: float32 [512, 8], replicated
- start_weight_grad: float32 [4, 512], replicated
Inputs may be any that keep to these rules, and one draw needn't show every extreme that they name: `audio`: audio samples.
All inputs are finite; a program needn't handle non-finite values.
Results may differ from a plain program's by a relative error of at most 0.015.
Values may be sent and summed in bfloat16 or wider, within the bound.
A program may use at most 128 MiB of HBM per device.

v0:
```python
import jax
import jax.numpy as jnp
from jax import lax
from jax.experimental.layout import Layout, with_layout_constraint
from jax.sharding import PartitionSpec as P

highest = lax.Precision.HIGHEST


def with_halo(block, sides, width):
    for axis, dim in sides:
        count = lax.axis_size(axis)
        forward = [(i, i + 1) for i in range(count - 1)]
        backward = [(target, source) for source, target in forward]
        low = lax.ppermute(
            lax.slice_in_dim(block, block.shape[dim] - width, None, axis=dim), axis, forward
        )
        high = lax.ppermute(lax.slice_in_dim(block, 0, width, axis=dim), axis, backward)
        block = jnp.concatenate([low, block, high], axis=dim)
    return block


def gated_unit(pre_act, channels):
    return jnp.tanh(pre_act[..., :channels]) * jax.nn.sigmoid(pre_act[..., channels:])


def gated_back(pre_act, upstream, channels):
    tangent = jnp.tanh(pre_act[..., :channels])
    switch = jax.nn.sigmoid(pre_act[..., channels:])
    return jnp.concatenate(
        [
            upstream * (1.0 - tangent * tangent) * switch,
            upstream * tangent * switch * (1.0 - switch),
        ],
        axis=-1,
    )


def project(values, weight):
    return jnp.einsum("cti,io->cto", values, weight, preferred_element_type=jnp.float32)


def dilated(padded, weight, spread, length):
    summed = None
    for tap_index in range(weight.shape[0]):
        window = padded[:, tap_index * spread : tap_index * spread + length]
        tap_term = project(window, weight[tap_index])
        summed = tap_term if summed is None else summed + tap_term
    return summed


def dilated_back(padded_grad, weight, spread, length):
    taps = weight.shape[0]
    summed = None
    for tap_index in range(taps):
        offset = (taps - 1 - tap_index) * spread
        window = padded_grad[:, offset : offset + length]
        tap_term = jnp.einsum(
            "cto,io->cti", window, weight[tap_index], preferred_element_type=jnp.float32
        )
        summed = tap_term if summed is None else summed + tap_term
    return summed


def shards(
    audio, mel_frames, start_weight, input_weight, cond_weight, res_weight, last_weight, end_weight
):
    clips_dev, group_size, frames_dev = audio.shape
    half_group = group_size // 2
    channels = start_weight.shape[1]
    layers = input_weight.shape[0]
    taps = input_weight.shape[1]
    scale_inv = 1.0 / (clips_dev * lax.axis_size("dp"))
    first_half = jnp.transpose(audio[:, :half_group], (0, 2, 1))
    second_half = jnp.transpose(audio[:, half_group:], (0, 2, 1))
    stored = []
    skip_sum = jnp.zeros((clips_dev, frames_dev, channels), jnp.float32)
    hidden = jnp.einsum("cth,hk->ctk", first_half, start_weight, precision=highest)
    for layer_index in range(layers):
        spread = 2**layer_index
        padded = with_halo(hidden.astype(jnp.bfloat16), (("tm", 1),), spread)
        pre_act = dilated(padded, input_weight[layer_index], spread, frames_dev) + project(
            mel_frames, cond_weight[layer_index]
        )
        gated_out = gated_unit(pre_act, channels).astype(jnp.bfloat16)
        stored.append((padded, pre_act, gated_out))
        if layer_index < layers - 1:
            mixed = project(gated_out, res_weight[layer_index])
            hidden = hidden + mixed[..., :channels]
            skip_sum = mixed[..., channels:]
        else:
            skip_sum = skip_sum + project(gated_out, last_weight)
    skip_b = skip_sum.astype(jnp.bfloat16)
    outputs = project(skip_b, end_weight)
    log_scale = outputs[..., :half_group]
    shift_term = outputs[..., half_group:]
    growth = jnp.exp(log_scale)
    latent_rows = growth * second_half + shift_term
    local_loss = (
        0.5 * jnp.sum(first_half * first_half)
        + 0.5 * jnp.sum(latent_rows * latent_rows)
        - jnp.sum(log_scale)
    ) * scale_inv
    grad_out = jnp.concatenate(
        [(latent_rows * growth * second_half - 1.0) * scale_inv, latent_rows * scale_inv], axis=-1
    ).astype(jnp.bfloat16)
    end_grad = jnp.einsum("cti,ctg->ig", skip_b, grad_out, preferred_element_type=jnp.float32)
    skip_back = jnp.einsum(
        "ctg,ig->cti", grad_out, end_weight, preferred_element_type=jnp.float32
    ).astype(jnp.bfloat16)
    state_back = jnp.zeros((clips_dev, frames_dev, channels), jnp.float32)
    in_grads = [None] * layers
    cond_grads = [None] * layers
    res_grads = [None] * (layers - 1)
    last_grad = None
    clip_sums = [None] * layers
    dp_size = lax.axis_size("dp")
    tm_size = lax.axis_size("tm")

    def by_clip_owner(grad):
        return grad.astype(jnp.bfloat16).reshape(dp_size, -1, grad.shape[1])

    def folded(grad):
        rows, columns = grad.shape
        halves = grad.astype(jnp.bfloat16).reshape(dp_size, 2, rows // dp_size // 2, columns)
        return jnp.transpose(halves, (0, 2, 1, 3)).reshape(rows // 2, 2 * columns)

    def unfolded(grad):
        rows, columns = grad.shape
        halves = grad.reshape(dp_size, rows // dp_size, 2, columns // 2)
        return jnp.transpose(halves, (0, 2, 1, 3)).reshape(2 * rows, columns // 2)

    for layer_index in reversed(range(layers)):
        spread = 2**layer_index
        padded, pre_act, gated_out = stored[layer_index]
        if layer_index == layers - 1:
            act_back = jnp.einsum(
                "ctj,ij->cti", skip_back, last_weight, preferred_element_type=jnp.float32
            )
            last_grad = jnp.einsum(
                "cti,ctj->ij", gated_out, skip_back, preferred_element_type=jnp.float32
            )
        else:
            joined = jnp.concatenate([state_back.astype(jnp.bfloat16), skip_back], axis=-1)
            act_back = jnp.einsum(
                "ctj,ij->cti", joined, res_weight[layer_index], preferred_element_type=jnp.float32
            )
            res_grads[layer_index] = jnp.einsum(
                "cti,ctj->ij", gated_out, joined, preferred_element_type=jnp.float32
            )
        pre_back = gated_back(pre_act, act_back, channels).astype(jnp.bfloat16)
        in_grads[layer_index] = [
                jnp.einsum(
                    "cti,cto->io",
                    padded[:, tap_index * spread : tap_index * spread + frames_dev],
                    pre_back,
                    preferred_element_type=jnp.float32,
                )
                for tap_index in range(taps)
            ]
        cond_grads[layer_index] = jnp.einsum(
            "ctm,cto->mo", mel_frames, pre_back, preferred_element_type=jnp.float32
        )
        grad_pad = with_halo(pre_back, (("tm", 1),), spread)
        state_back = state_back + dilated_back(
            grad_pad, input_weight[layer_index], spread, frames_dev
        )
        pieces = in_grads[layer_index] + [cond_grads[layer_index]]
        if layer_index == layers - 1:
            pieces.append(folded(last_grad))
        else:
            pieces.append(res_grads[layer_index])
        packed = jnp.concatenate([by_clip_owner(piece) for piece in pieces], axis=1)
        packed = with_layout_constraint(packed, Layout(major_to_minor=(0, 1, 2)))
        clip_sums[layer_index] = lax.psum_scatter(
            packed, "dp", scatter_dimension=0, tiled=True
        )[0]
    start_grad = jnp.einsum("cth,ctk->hk", first_half, state_back, precision=highest)
    first_back = (
        jnp.einsum("ctk,hk->cth", state_back, start_weight, precision=highest)
        + first_half * scale_inv
    )
    audio_grad = jnp.transpose(
        jnp.concatenate([first_back, latent_rows * growth * scale_inv], axis=-1), (0, 2, 1)
    )
    latent = jnp.transpose(latent_rows, (0, 2, 1))
    small = jnp.concatenate(
        [end_grad.reshape(-1), start_grad.reshape(-1), local_loss.reshape(1)]
    )
    small = lax.psum(lax.psum(small, "tm"), "dp")
    end_total = small[: end_grad.size].reshape(end_grad.shape)
    start_total = small[end_grad.size : end_grad.size + start_grad.size].reshape(start_grad.shape)
    batch_loss = small[-1]
    grad_rows = clip_sums[-1].shape[0] - channels // dp_size // 2
    last_parts = lax.all_gather(clip_sums[-1][grad_rows:], "tm")
    last_rows = jnp.sum(last_parts.astype(jnp.float32), axis=0).astype(jnp.bfloat16)
    last_total = unfolded(lax.all_gather(last_rows, "dp", tiled=True)).astype(jnp.float32)
    clip_sums = clip_sums[:-1] + [clip_sums[-1][:grad_rows]]
    clip_sums, end_total, start_total, batch_loss, last_total = lax.optimization_barrier(
        (clip_sums, end_total, start_total, batch_loss, last_total)
    )
    rows_all = jnp.concatenate(clip_sums, axis=0)
    width = rows_all.shape[1] // tm_size
    by_frame_owner = jnp.stack(
        [rows_all[:, at * width : (at + 1) * width] for at in range(tm_size)]
    )
    by_frame_owner = with_layout_constraint(by_frame_owner, Layout(major_to_minor=(0, 1, 2)))
    mine = lax.psum_scatter(by_frame_owner, "tm", scatter_dimension=0, tiled=True)[0]
    mine = mine.astype(jnp.float32)
    in_sums, cond_sums, res_sums, taken = [], [], [], 0
    for layer_index in range(layers):
        rows = taps * channels // dp_size
        in_sums.append(mine[taken : taken + rows].reshape(taps, channels // dp_size, width))
        taken += rows
        rows = mel_frames.shape[2] // dp_size
        cond_sums.append(mine[taken : taken + rows])
        taken += rows
        if layer_index < layers - 1:
            rows = channels // dp_size
            res_sums.append(mine[taken : taken + rows])
            taken += rows
    in_grad = jnp.stack(in_sums)
    cond_grad = jnp.stack(cond_sums)
    res_grad = jnp.stack(res_sums)
    return (
        latent,
        audio_grad,
        batch_loss,
        in_grad,
        cond_grad,
        res_grad,
        last_total,
        end_total,
        start_total,
    )


def solution(mesh):
    return jax.shard_map(
        shards,
        mesh=mesh,
        in_specs=(P("dp", None, "tm"), P("dp", "tm", None), P(), P(), P(), P(), P(), P()),
        out_specs=(
            P("dp", None, "tm"),
            P("dp", None, "tm"),
            P(),
            P(None, None, "dp", "tm"),
            P(None, "dp", "tm"),
            P(None, "dp", "tm"),
            P(),
            P(),
            P(),
        ),
        check_vma=False,
    )
```

profile of v0, /device:TPU:0, one launch (start us, length us, event | category | flops | bytes accessed | tf_op | source)
XLA Modules:
  0.0 224.9 jit_solution(7631894428275843401)
XLA Ops:
  7.3 2.3 %fusion.105 = (bf16[3,256,512]{2,1,0:T(8,128)(2,1)S(1)}, f32[3,256,512]{2,1,0:T(8,128)S(1)}) fusion(f32[4,512]{1,0:T(4,128)} %param.10, f32[3,8,256]{2,1,0:T(8,128)} %param.8), kind=kOutput, calls=%fused_computation.180 | convolution fusion | flops 19267584 | bytes 2379776 | tf_op jit(solution)/shard_map/cth,hk->ctk/dot_general | solution.py:78
  11.0 5.9 %collective-permute-start = (bf16[3,1,512]{2,1,0:T(2,128)(2,1)S(1)}, bf16[3,1,512]{2,1,0:T(2,128)(2,1)S(1)}, u32[]{:S(2)}, u32[]{:S(2)}) collective-permute-start(bf16[3,1,512]{2,1,0:T(2,128)(2,1)S(1)} %get-tuple-element.65), channel_id=1, source_target_pairs={{0,1},{1,2},{2,3},{4,5},{5,6},{6,7},{8,9},{9,10},{10,11},{12,13},{... | collective-permute-start | bytes 9224 | tf_op jit(solution)/shard_map/ppermute | solution.py:15
  16.8 2.7 %fusion.16 = f32[3,256,1024]{2,1,0:T(8,128)S(1)} fusion(bf16[3,256,640]{2,1,0:T(8,128)(2,1)S(1)} %copy-done.25, bf16[2,640,1024]{2,1,0:T(8,128)(2,1)} %param.12), kind=kOutput, calls=%fused_computation.54 | convolution fusion | flops 1006632960 | bytes 5439488 | tf_op jit(solution)/shard_map/cti,io->cto/dot_general | solution.py:40
  27.1 3.9 %collective-permute-start.2 = (bf16[3,2,512]{2,1,0:T(2,128)(2,1)S(1)}, bf16[3,2,512]{2,1,0:T(2,128)(2,1)S(1)}, u32[]{:S(2)}, u32[]{:S(2)}) collective-permute-start(bf16[3,2,512]{2,1,0:T(2,128)(2,1)S(1)} %get-tuple-element.63), channel_id=1, source_target_pairs={{0,1},{1,2},{2,3},{4,5},{5,6},{6,7},{8,9},{9,10},{10,11},{12,13},{... | collective-permute-start | bytes 18440 | tf_op jit(solution)/shard_map/ppermute | solution.py:15
  34.5 3.0 %collective-permute-done.3 = bf16[3,2,512]{2,1,0:T(2,128)(2,1)S(1)} collective-permute-done((bf16[3,2,512]{2,1,0:T(2,128)(2,1)S(1)}, bf16[3,2,512]{2,1,0:T(2,128)(2,1)S(1)}, u32[]{:S(2)}, u32[]{:S(2)}) %collective-permute-start.3) | collective-permute-done | bytes 6176 | tf_op jit(solution)/shard_map/ppermute | solution.py:18
  43.5 2.0 bitcast_convert_fusion.3
  45.5 2.3 %bitcast_convert_fusion = bf16[1024,640]{0,1:T(8,128)(2,1)} fusion(bf16[3,256,640]{2,1,0:T(8,128)(2,1)S(1)} %copy-done.26, bf16[3,256,512]{2,1,0:T(8,128)(2,1)S(1)} %get-tuple-element.53, bf16[3,256,512]{2,1,0:T(8,128)(2,1)S(1)} %get-tuple-element.52), kind=kOutput, calls=%fused_computation.2 | convolution fusion | flops 1010434048 | bytes 3866624 | tf_op jit(solution)/shard_map/ctm,cto->mo/dot_general | solution.py:161
  49.1 2.2 reshape_reshape.3
  51.4 2.4 %bitcast_convert_fusion.4 = bf16[512,1024]{1,0:T(8,128)(2,1)S(1)} fusion(bf16[3,256,512]{2,1,0:T(8,128)(2,1)S(1)} %fusion.11, bf16[3,2,512]{2,1,0:T(2,128)(2,1)S(1)} %collective-permute-done.2, bf16[3,256,512]{2,1,0:T(8,128)(2,1)} %copy-done.15, bf16[3,256,512]{2,1,0:T(8,128)(2,1)} %copy-done.12), kind=kOutput, calls=%fused_computation.6 | convolution fusion | flops 810549248 | bytes 3414016 | tf_op jit(solution)/shard_map/cti,cto->io/dot_general | solution.py:153
  64.6 2.2 fusion.44
  66.8 5.0 %collective-permute-start.5 = (bf16[3,2,1024]{2,1,0:T(2,128)(2,1)S(1)}, bf16[3,2,1024]{2,1,0:T(2,128)(2,1)S(1)}, u32[]{:S(2)}, u32[]{:S(2)}) collective-permute-start(bf16[3,2,1024]{2,1,0:T(2,128)(2,1)S(1)} %get-tuple-element.56), channel_id=1, source_target_pairs={{0,1},{1,2},{2,3},{4,5},{5,6},{6,7},{8,9},{9,10},{10,11},{12,13},{... | collective-permute-start | bytes 36872 | tf_op jit(solution)/shard_map/ppermute | solution.py:15
  71.8 2.4 %fusion.6 = f32[3,256,512]{2,1,0:T(8,128)S(1)} fusion(bf16[3,2,1024]{2,1,0:T(2,128)(2,1)S(1)} %collective-permute-done.4, bf16[3,256,512]{2,1,0:T(8,128)(2,1)S(1)} %copy-done.17, bf16[3,256,512]{2,1,0:T(8,128)(2,1)S(1)} %copy-done.14, bf16[2,3,512,1024]{3,2,1,0:T(8,128)(2,1)} %param.11), kind=kOutput, calls=%fused_computation.24 | convolution fusion | flops 810024960 | bytes 4206592 | tf_op jit(solution)/shard_map/cto,io->cti/dot_general | solution.py:58
  74.2 3.6 %fusion.106 = (bf16[3,256,512]{2,1,0:T(8,128)(2,1)S(1)}, f32[3,256,512]{2,1,0:T(8,128)}) fusion(bf16[2,3,512,1024]{3,2,1,0:T(8,128)(2,1)} %param.11, bf16[3,2,1024]{2,1,0:T(2,128)(2,1)S(1)} %collective-permute-done.5, bf16[3,256,512]{2,1,0:T(8,128)(2,1)S(1)} %copy-done.17, bf16[3,256,512]{2,1,0:T(8,128)(2,1)S(1)} %copy-done.14, ...), kind=kOutput, calls=%fused_computation.181 | convolution fusion | flops 811204608 | bytes 8138752 | tf_op jit(solution)/shard_map/cto,io->cti/dot_general | solution.py:58
  95.9 2.5 %fusion.30 = f32[3,256,512]{2,1,0:T(8,128)S(1)} fusion(bf16[2,3,512,1024]{3,2,1,0:T(8,128)(2,1)} %param.11, bf16[3,256,512]{2,1,0:T(8,128)(2,1)} %copy-done.10, bf16[3,256,512]{2,1,0:T(8,128)(2,1)S(1)} %get-tuple-element.50), kind=kOutput, calls=%fused_computation.68 | convolution fusion | flops 808452096 | bytes 4194304 | tf_op jit(solution)/shard_map/cto,io->cti/dot_general | solution.py:58
  98.4 5.0 %collective-permute-start.7 = (bf16[3,1,1024]{2,1,0:T(2,128)(2,1)S(1)}, bf16[3,1,1024]{2,1,0:T(2,128)(2,1)S(1)}, u32[]{:S(2)}, u32[]{:S(2)}) collective-permute-start(bf16[3,1,1024]{2,1,0:T(2,128)(2,1)S(1)} %get-tuple-element.54), channel_id=1, source_target_pairs={{0,1},{1,2},{2,3},{4,5},{5,6},{6,7},{8,9},{9,10},{10,11},{12,13},{... | collective-permute-start | bytes 18440 | tf_op jit(solution)/shard_map/ppermute | solution.py:15
  103.4 2.2 fusion.2
  105.6 2.3 %add_add_fusion.2 = f32[3,256,512]{2,1,0:T(8,128)S(1)} fusion(f32[3,256,512]{2,1,0:T(8,128)S(1)} %copy-done.28, f32[3,256,512]{2,1,0:T(8,128)S(1)} %fusion.2, f32[3,256,512]{2,1,0:T(8,128)S(1)} %fusion.30, bf16[3,1,1024]{2,1,0:T(2,128)(2,1)S(1)} %collective-permute-done.7, bf16[3,256,512]{2,1,0:T(8,128)(2,1)S(1)} %copy-done.11, ...), kind=kOutput, calls=%fused_computation.44 | convolution fusion | flops 811204608 | bytes 8919040 | tf_op jit(solution)/shard_map/cto,io->cti/dot_general | solution.py:58
  108.9 18.8 %psum.14 = f32[6145]{0:T(1024)S(1)} all-reduce(f32[6145]{0:T(1024)S(1)} %pad_maximum_fusion.40), channel_id=1, replica_groups=mesh['dp'=8,'tm'=4] {'tm'}, use_global_device_ids=true, to_apply=%region_5.0 | all-reduce | flops 6145 | bytes 49160 | tf_op jit(solution)/shard_map/psum | solution.py:190
  127.7 23.0 %psum.15 = f32[6145]{0:T(1024)S(1)} all-reduce(f32[6145]{0:T(1024)S(1)} %psum.14), channel_id=1, replica_groups=mesh['dp'=8,'tm'=4] {'dp'}, use_global_device_ids=true, to_apply=%region_6.0 | all-reduce | flops 6145 | bytes 49160 | tf_op jit(solution)/shard_map/psum | solution.py:190
  152.8 13.9 %all_gather.7 = bf16[4,32,1024]{2,1,0:T(8,128)(2,1)S(1)} all-gather(bf16[1,32,1024]{2,1,0:T(8,128)(2,1)S(1)} %slice.256), channel_id=1, replica_groups=mesh['dp'=8,'tm'=4] {'tm'}, dimensions={0}, use_global_device_ids=true | all-gather | bytes 327680 | tf_op jit(solution)/shard_map/all_gather | solution.py:195
  166.8 11.8 %all_gather.8 = bf16[256,1024]{1,0:T(8,128)(2,1)S(1)} all-gather(bf16[32,1024]{1,0:T(8,128)(2,1)S(1)} %reduce_sum.42), channel_id=1, replica_groups=mesh['dp'=8,'tm'=4] {'dp'}, dimensions={0}, use_global_device_ids=true | all-gather | bytes 589824 | tf_op jit(solution)/shard_map/all_gather | solution.py:197
  178.6 1.9 reshape.111
  180.5 2.4 %copy.67 = f32[8,2,32,512]{3,2,1,0:T(8,128)} copy(f32[8,2,32,512]{3,1,2,0:T(2,128)} %bitcast.199) | data formatting | bytes 2097152 | tf_op jit(solution)/shard_map/convert_element_type | solution.py:197
  188.3 25.4 %reduce-scatter.8.cloned.1.call-done = bf16[1,608,256]{2,1,0:T(8,128)(2,1)} async-done(((bf16[4,608,256]{2,1,0:T(8,128)(2,1)}), bf16[1,608,256]{2,1,0:T(8,128)(2,1)}) %reduce-scatter.8.cloned.1.call-update) | async-done | bytes 311312 | tf_op jit(solution)/shard_map/reduce_scatter | solution.py:208
  (147 shorter events, 59.4 us)
Async XLA Ops:
  7.2 18.5 %copy-start = (bf16[1,512,1024]{2,1,0:T(8,128)(2,1)S(1)}, bf16[1,512,1024]{2,1,0:T(8,128)(2,1)}, u32[]{:S(2)}) copy-start(bf16[1,512,1024]{2,1,0:T(8,128)(2,1)} %param.13) | copy-start | bytes 3145732
  7.2 9.6 %copy-start.25 = (bf16[3,256,640]{2,1,0:T(8,128)(2,1)S(1)}, bf16[3,256,640]{2,1,0:T(8,128)(2,1)}, u32[]{:S(2)}) copy-start(bf16[3,256,640]{2,1,0:T(8,128)(2,1)} %param.9) | copy-start | bytes 2949124
  7.2 144.8 %reduce-scatter.6.cloned.1.call-start = ((), (), s32[]{:S(2)}) async-start(), calls=%async_computation.4 | async-start | bytes 5603328 | tf_op jit(solution)/shard_map/reduce_scatter | solution.py:175
  7.2 13.7 %slice-start = ((s8[6291456]{0:T(1024)(128)(4,1)}), s8[4194304]{0:T(1024)(128)(4,1)S(1)}, s32[]{:S(2)}) async-start(s8[6291456]{0:T(1024)(128)(4,1)} %bitcast.197), calls=%async_computation.6 | async-start | bytes 8388608
  9.6 13.3 %collective-permute-start.1 = (bf16[3,1,512]{2,1,0:T(2,128)(2,1)S(1)}, bf16[3,1,512]{2,1,0:T(2,128)(2,1)S(1)}, u32[]{:S(2)}, u32[]{:S(2)}) collective-permute-start(bf16[3,1,512]{2,1,0:T(2,128)(2,1)S(1)} %get-tuple-element.64), channel_id=1, source_target_pairs={{1,0},{2,1},{3,2},{5,4},{6,5},{7,6},{9,8},{10,9},{11,10},{13,12},{... | collective-permute-start | bytes 9224 | tf_op jit(solution)/shard_map/ppermute | solution.py:18
  10.9 8.6 %copy-start.24 = (bf16[2,640,1024]{2,1,0:T(8,128)(2,1)S(1)}, bf16[2,640,1024]{2,1,0:T(8,128)(2,1)}, u32[]{:S(2)}) copy-start(bf16[2,640,1024]{2,1,0:T(8,128)(2,1)} %param.12) | copy-start | bytes 7864324
  10.9 10.0 %slice-start.1 = ((s8[6291456]{0:T(1024)(128)(4,1)}), s8[2097152]{0:T(1024)(128)(4,1)S(1)}, s32[]{:S(2)}) async-start(s8[6291456]{0:T(1024)(128)(4,1)} %bitcast.197), calls=%async_computation.7 | async-start | bytes 4194304
  11.0 11.0 %collective-permute-start = (bf16[3,1,512]{2,1,0:T(2,128)(2,1)S(1)}, bf16[3,1,512]{2,1,0:T(2,128)(2,1)S(1)}, u32[]{:S(2)}, u32[]{:S(2)}) collective-permute-start(bf16[3,1,512]{2,1,0:T(2,128)(2,1)S(1)} %get-tuple-element.65), channel_id=1, source_target_pairs={{0,1},{1,2},{2,3},{4,5},{5,6},{6,7},{8,9},{9,10},{10,11},{12,13},{... | collective-permute-start | bytes 9224 | tf_op jit(solution)/shard_map/ppermute | solution.py:15
  27.1 6.4 %collective-permute-start.2 = (bf16[3,2,512]{2,1,0:T(2,128)(2,1)S(1)}, bf16[3,2,512]{2,1,0:T(2,128)(2,1)S(1)}, u32[]{:S(2)}, u32[]{:S(2)}) collective-permute-start(bf16[3,2,512]{2,1,0:T(2,128)(2,1)S(1)} %get-tuple-element.63), channel_id=1, source_target_pairs={{0,1},{1,2},{2,3},{4,5},{5,6},{6,7},{8,9},{9,10},{10,11},{12,13},{... | collective-permute-start | bytes 18440 | tf_op jit(solution)/shard_map/ppermute | solution.py:15
  32.0 5.5 %collective-permute-start.3 = (bf16[3,2,512]{2,1,0:T(2,128)(2,1)S(1)}, bf16[3,2,512]{2,1,0:T(2,128)(2,1)S(1)}, u32[]{:S(2)}, u32[]{:S(2)}) collective-permute-start(bf16[3,2,512]{2,1,0:T(2,128)(2,1)S(1)} %get-tuple-element.62), channel_id=1, source_target_pairs={{1,0},{2,1},{3,2},{5,4},{6,5},{7,6},{9,8},{10,9},{11,10},{13,12},{... | collective-permute-start | bytes 18440 | tf_op jit(solution)/shard_map/ppermute | solution.py:18
  42.9 2.6 %copy-start.12 = (bf16[3,256,512]{2,1,0:T(8,128)(2,1)}, bf16[3,256,512]{2,1,0:T(8,128)(2,1)S(1)}, u32[]{:S(2)}) copy-start(bf16[3,256,512]{2,1,0:T(8,128)(2,1)S(1)} %get-tuple-element.52) | copy-start | bytes 2359300
  42.9 2.6 %copy-start.15 = (bf16[3,256,512]{2,1,0:T(8,128)(2,1)}, bf16[3,256,512]{2,1,0:T(8,128)(2,1)S(1)}, u32[]{:S(2)}) copy-start(bf16[3,256,512]{2,1,0:T(8,128)(2,1)S(1)} %get-tuple-element.53) | copy-start | bytes 2359300
  61.3 121.7 %reduce-scatter.4.cloned.1.call-start = ((), (), s32[]{:S(2)}) async-start(), calls=%async_computation.3 | async-start | bytes 6193152 | tf_op jit(solution)/shard_map/reduce_scatter | solution.py:175
  63.3 8.5 %collective-permute-start.4 = (bf16[3,2,1024]{2,1,0:T(2,128)(2,1)S(1)}, bf16[3,2,1024]{2,1,0:T(2,128)(2,1)S(1)}, u32[]{:S(2)}, u32[]{:S(2)}) collective-permute-start(bf16[3,2,1024]{2,1,0:T(2,128)(2,1)S(1)} %get-tuple-element.57), channel_id=1, source_target_pairs={{1,0},{2,1},{3,2},{5,4},{6,5},{7,6},{9,8},{10,9},{11,10},{13,12},{... | collective-permute-start | bytes 36872 | tf_op jit(solution)/shard_map/ppermute | solution.py:18
  66.8 7.4 %collective-permute-start.5 = (bf16[3,2,1024]{2,1,0:T(2,128)(2,1)S(1)}, bf16[3,2,1024]{2,1,0:T(2,128)(2,1)S(1)}, u32[]{:S(2)}, u32[]{:S(2)}) collective-permute-start(bf16[3,2,1024]{2,1,0:T(2,128)(2,1)S(1)} %get-tuple-element.56), channel_id=1, source_target_pairs={{0,1},{1,2},{2,3},{4,5},{5,6},{6,7},{8,9},{9,10},{10,11},{12,13},{... | collective-permute-start | bytes 36872 | tf_op jit(solution)/shard_map/ppermute | solution.py:15
  74.2 3.6 %copy-start.2 = (f32[3,256,1024]{2,1,0:T(8,128)S(1)}, f32[3,256,1024]{2,1,0:T(8,128)}, u32[]{:S(2)}) copy-start(f32[3,256,1024]{2,1,0:T(8,128)} %copy-done.1) | copy-start | bytes 9437188
  74.2 3.6 %copy-start.9 = (bf16[3,256,512]{2,1,0:T(8,128)(2,1)S(1)}, bf16[3,256,512]{2,1,0:T(8,128)(2,1)}, u32[]{:S(2)}) copy-start(bf16[3,256,512]{2,1,0:T(8,128)(2,1)} %copy-done.8) | copy-start | bytes 2359300
  79.4 6.5 %copy-start.10 = (bf16[3,256,512]{2,1,0:T(8,128)(2,1)}, bf16[3,256,512]{2,1,0:T(8,128)(2,1)S(1)}, u32[]{:S(2)}) copy-start(bf16[3,256,512]{2,1,0:T(8,128)(2,1)S(1)} %get-tuple-element.51) | copy-start | bytes 2359300
  91.1 122.6 %reduce-scatter.8.cloned.1.call-start = ((), (), s32[]{:S(2)}) async-start(), calls=%async_computation.5 | async-start | bytes 1556480 | tf_op jit(solution)/shard_map/reduce_scatter | solution.py:208
  94.4 8.9 %copy-start.11 = (bf16[3,256,512]{2,1,0:T(8,128)(2,1)S(1)}, bf16[3,256,512]{2,1,0:T(8,128)(2,1)}, u32[]{:S(2)}) copy-start(bf16[3,256,512]{2,1,0:T(8,128)(2,1)} %copy-done.10) | copy-start | bytes 2359300
  94.5 8.9 %collective-permute-start.6 = (bf16[3,1,1024]{2,1,0:T(2,128)(2,1)S(1)}, bf16[3,1,1024]{2,1,0:T(2,128)(2,1)S(1)}, u32[]{:S(2)}, u32[]{:S(2)}) collective-permute-start(bf16[3,1,1024]{2,1,0:T(2,128)(2,1)S(1)} %get-tuple-element.55), channel_id=1, source_target_pairs={{1,0},{2,1},{3,2},{5,4},{6,5},{7,6},{9,8},{10,9},{11,10},{13,12},{... | collective-permute-start | bytes 18440 | tf_op jit(solution)/shard_map/ppermute | solution.py:18
  98.4 7.3 %copy-start.28 = (f32[3,256,512]{2,1,0:T(8,128)S(1)}, f32[3,256,512]{2,1,0:T(8,128)}, u32[]{:S(2)}) copy-start(f32[3,256,512]{2,1,0:T(8,128)} %get-tuple-element.78) | copy-start | bytes 4718596
  98.4 7.2 %collective-permute-start.7 = (bf16[3,1,1024]{2,1,0:T(2,128)(2,1)S(1)}, bf16[3,1,1024]{2,1,0:T(2,128)(2,1)S(1)}, u32[]{:S(2)}, u32[]{:S(2)}) collective-permute-start(bf16[3,1,1024]{2,1,0:T(2,128)(2,1)S(1)} %get-tuple-element.54), channel_id=1, source_target_pairs={{0,1},{1,2},{2,3},{4,5},{5,6},{6,7},{8,9},{9,10},{10,11},{12,13},{... | collective-permute-start | bytes 18440 | tf_op jit(solution)/shard_map/ppermute | solution.py:15
  180.5 2.5 %copy-start.18 = (bf16[1,304,1024]{2,1,0:T(8,128)(2,1)S(1)}, bf16[1,304,1024]{2,1,0:T(8,128)(2,1)}, u32[]{:S(2)}) copy-start(bf16[1,304,1024]{2,1,0:T(8,128)(2,1)} %reduce-scatter.6.cloned.1.call-done) | copy-start | bytes 1867780
  (18 other events, 26.0 us)
Sparse Core Ops, SparseCore 0:
  61.4 54.3 reduce-scatter.5
  119.3 59.8 reduce-scatter.3
  185.7 27.9 reduce-scatter.7
where the time goes:
time: 226 us; the launch traced here: 225 us
  blocking collectives  67.5 us (30%)
  matrix products  48.9 us (22%)
  local copies, waits for them, and re-layouts  31 us (14%)
  waiting for transfers between devices  28.5 us (13%)
  starting transfers between devices  25.3 us (11%)
  between operations  16.4 us (7%)
  other arithmetic  7.3 us (3%)
    psum x2, blocking collectives, shards(): small = lax.psum(lax.psum(small, 'tm'), 'dp')  41.7 us
    reduce_scatter x1, waiting for transfers between devices, shards(): lax.psum_scatter(by_frame_owner, 'tm', scatter_dimension=0, tiled=True)[0]  25.4 us
    ppermute x4, starting transfers between devices, with_halo(): lax.ppermute(lax.slice_in_dim(block, block.shape[dim] - width, None, axis...  19.7 us
    unnamed x73, local copies, waits for them, and re-layouts  15.4 us
    dot_general x6, matrix products, dilated_back(): jnp.einsum('cto,io->cti', window, weight[tap_index], preferred_element_ty...  15.2 us
    all_gather x1, blocking collectives, shards(): last_parts = lax.all_gather(clip_sums[-1][grad_rows:], 'tm')  13.9 us
    dot_general x11, matrix products, project(): jnp.einsum('cti,io->cto', values, weight, preferred_element_type=jnp.floa...  11.9 us
    all_gather x1, blocking collectives, shards(): lax.all_gather(last_rows, 'dp', tiled=True)  11.8 us
  transfers between devices with their start and end apart: 11, of which 2 were waited for; matrix products, arithmetic and copies ran while one was open for 21% of the time, Pallas kernels for 0%

commit v1 on v0

v1 whole, which is shorter than its diff:
```python
import itertools

import jax
import jax.numpy as jnp
from jax import lax
from jax.experimental import pallas as pl
from jax.experimental.pallas import tpu as pltpu
from jax.sharding import PartitionSpec as P

F32 = jnp.float32
BF16 = jnp.bfloat16
HIGHEST = lax.Precision.HIGHEST
MESH = pl.DeviceIdType.MESH
EDGE = 8
BLOCK = 256
LANES = 128


def dot(a, b, dims=((1,), (0,)), precision=None):
    return lax.dot_general(
        a, b, (dims, ((), ())), precision=precision, preferred_element_type=F32
    )


def round_up(value, unit):
    return -(-value // unit) * unit


class Plan:
    def __init__(self, mesh, audio, mel, start_weight, input_weight):
        self.dp, self.tm = mesh.shape["dp"], mesh.shape["tm"]
        self.bits = self.dp.bit_length() - 1
        self.clips, self.group, self.frames = audio.shape
        self.half = self.group // 2
        self.cond = mel.shape[2]
        self.channels = start_weight.shape[1]
        self.layers, self.taps = input_weight.shape[:2]
        self.wide = 2 * self.channels
        self.rows = self.clips * self.frames
        self.all_rows = self.rows + self.clips * 2 * EDGE
        self.pad_rows = round_up(self.all_rows, LANES)
        self.own_ch = self.channels // self.dp
        self.own_cond = self.cond // self.dp
        self.width = self.wide // self.tm
        order = list(range(self.bits))
        self.first = order
        self.second = order[:1] + order[1:][::-1]
        tap_pair = tuple(range(self.taps - 1))
        rest = (self.taps - 1, "cond")
        self.chunks = [
            (1, tap_pair, self.wide, self.first),
            (1, rest, self.wide, self.second),
            (0, ("res",), self.channels, self.second),
            (0, tap_pair, self.wide, self.first),
            (0, rest, self.wide, self.second),
        ]

    def part_rows(self, part):
        return self.own_cond if part == "cond" else self.own_ch

    def chunk_rows(self, chunk):
        return round_up(sum(self.part_rows(part) for part in chunk[1]), 16)


def kernel(plan, *refs):
    p = plan
    n_in, n_out = 8, 9
    (audio_h, mel_h, start_w, win_h, cond_h, res_h, last_h, end_w) = refs[:n_in]
    (
        latent_o, audio_o, loss_o, in_o, cond_o, res_o, last_o, end_o, start_o
    ) = refs[n_in : n_in + n_out]
    s = refs[n_in + n_out]
    me_dp, me_tm = lax.axis_index("dp"), lax.axis_index("tm")
    bit_of = [(me_dp // 2**b) % 2 for b in range(p.bits)]
    ch, rows, all_rows, fr = p.channels, p.rows, p.all_rows, p.frames
    ext = fr + 2 * EDGE
    n_blocks = ch // BLOCK

    def partner(b):
        return {"dp": me_dp + (2**b) * (1 - 2 * bit_of[b]), "tm": me_tm}

    def peer(step):
        return {"dp": me_dp, "tm": lax.rem(me_tm + step, p.tm)}

    loads = {}

    def load(name, src, dst, index):
        copy = pltpu.make_async_copy(src, dst, s["load_sem"].at[index])
        copy.start()
        loads[name] = copy

    load("audio", audio_h, s["audio"], 0)
    for clip in range(p.clips):
        load(
            f"mel{clip}", mel_h.at[clip], s["mel"].at[pl.ds(clip * fr, fr)], 1 + clip
        )
    base = 1 + p.clips
    for layer in range(p.layers):
        load(f"win{layer}", win_h.at[layer], s["win"].at[layer], base + 2 * layer)
        load(f"cond{layer}", cond_h.at[layer], s["cond"].at[layer], base + 2 * layer + 1)
        if layer == 0:
            load("res", res_h, s["res"], base + 2 * p.layers)
            load("last", last_h, s["last"], base + 2 * p.layers + 1)

    barrier = pltpu.get_barrier_semaphore()
    for b in range(p.bits):
        pl.semaphore_signal(barrier, 1, device_id=partner(b), device_id_type=MESH)
    for step in range(1, p.tm):
        pl.semaphore_signal(barrier, 1, device_id=peer(step), device_id_type=MESH)
    pl.semaphore_wait(barrier, p.bits + p.tm - 1)

    has_low, has_high = me_tm > 0, me_tm < p.tm - 1

    def halo_copies(slot):
        device = {"dp": me_dp, "tm": me_tm + 1 if slot == 0 else me_tm - 1}
        mel_at = fr - 2 * EDGE if slot == 0 else 0
        audio_at = fr - LANES if slot == 0 else 0
        return [
            pltpu.make_async_remote_copy(
                audio_h.at[:, :, pl.ds(audio_at, LANES)],
                s["audio_halo"].at[slot],
                s["halo_send"].at[slot, 0], s["halo_recv"].at[slot, 0],
                device_id=device, device_id_type=MESH,
            ),
            pltpu.make_async_remote_copy(
                mel_h.at[:, pl.ds(mel_at, 2 * EDGE)],
                s["mel_halo"].at[slot],
                s["halo_send"].at[slot, 1], s["halo_recv"].at[slot, 1],
                device_id=device, device_id_type=MESH,
            ),
        ]

    to_high, to_low = halo_copies(0), halo_copies(1)

    @pl.when(has_high)
    def _():
        for copy in to_high:
            copy.start()

    @pl.when(has_low)
    def _():
        for copy in to_low:
            copy.start()

    def halo_wait(index):
        @pl.when(has_low)
        def _():
            to_high[index].wait_recv()

        @pl.when(has_high)
        def _():
            to_low[index].wait_recv()

    def free_bits(order, stage):
        done = set(order[:stage])
        return [b for b in reversed(range(p.bits)) if b not in done]

    def g_index(values):
        return tuple(values[b] for b in reversed(range(p.bits)))

    def g_blocks(chunk_id, stage, other):
        order = p.chunks[chunk_id][3]
        bit = order[stage]
        free = free_bits(order, stage + 1)
        for combo in itertools.product((0, 1), repeat=len(free)):
            values = {b: bit_of[b] for b in order[:stage]}
            values[bit] = 1 - bit_of[bit] if other else bit_of[bit]
            values.update(zip(free, combo))
            yield values

    def recv_index(order, stage, values):
        return tuple(values[b] for b in free_bits(order, stage + 1))

    def add_block(chunk_id, stages, values):
        order = p.chunks[chunk_id][3]
        acc = s["grad"][chunk_id]
        at = g_index(values)
        height = acc.shape[-2]

        @pl.loop(0, height // 16)
        def _(r):
            where = (pl.ds(pl.multiple_of(r * 16, 16), 16),)
            total = acc[at + where].astype(F32)
            for stage in range(stages):
                buf = s["recv"][chunk_id][stage]
                total += buf[recv_index(order, stage, values) + where].astype(F32)
            acc[at + where] = total.astype(BF16)

    def stage_copy(chunk_id, stage):
        order = p.chunks[chunk_id][3]
        bit = order[stage]
        values = {b: slice(None) for b in range(p.bits)}
        values.update({b: bit_of[b] for b in order[:stage]})
        values[bit] = 1 - bit_of[bit]
        return pltpu.make_async_remote_copy(
            s["grad"][chunk_id].at[g_index(values)],
            s["recv"][chunk_id][stage],
            s["dp_send"].at[chunk_id, stage], s["dp_recv"].at[chunk_id, stage],
            device_id=partner(bit), device_id_type=MESH,
        )

    def dp_send(chunk_id, stage):
        if stage:
            stage_copy(chunk_id, stage - 1).wait_recv()
            for values in g_blocks(chunk_id, stage, True):
                add_block(chunk_id, stage, values)
        stage_copy(chunk_id, stage).start()

    def owners(chunk_id):
        return p.chunks[chunk_id][2] // p.width

    def tm_copy(chunk_id, step):
        target = lax.rem(me_tm + step, p.tm)
        at = g_index({b: bit_of[b] for b in range(p.bits)})
        place = lax.rem(target, owners(chunk_id))
        cols = pl.ds(pl.multiple_of(place * p.width, LANES), p.width)
        return pltpu.make_async_remote_copy(
            s["grad"][chunk_id].at[at + (slice(None), cols)],
            s["tm_recv_buf"][chunk_id].at[step - 1],
            s["tm_send"].at[chunk_id, step - 1], s["tm_recv"].at[chunk_id, step - 1],
            device_id={"dp": me_dp, "tm": target}, device_id_type=MESH,
        )

    def when_owner(chunk_id, position, run):
        if owners(chunk_id) == p.tm:
            run()
        else:
            pl.when(position < owners(chunk_id))(run)

    def tm_send(chunk_id):
        stage_copy(chunk_id, p.bits - 1).wait_recv()
        add_block(chunk_id, p.bits, {b: bit_of[b] for b in range(p.bits)})
        for step in range(1, p.tm):
            when_owner(
                chunk_id, lax.rem(me_tm + step, p.tm), tm_copy(chunk_id, step).start
            )

    def finish(chunk_id):
        layer, parts, _, _ = p.chunks[chunk_id]
        at = g_index({b: bit_of[b] for b in range(p.bits)})

        def run():
            for step in range(1, p.tm):
                tm_copy(chunk_id, step).wait_recv()
            cols = pl.ds(pl.multiple_of(me_tm * p.width, LANES), p.width)
            total = s["grad"][chunk_id][at + (slice(None), cols)].astype(F32)
            for step in range(1, p.tm):
                total += s["tm_recv_buf"][chunk_id][step - 1].astype(F32)
            row = 0
            for part in parts:
                high = p.part_rows(part)
                piece = total[row : row + high]
                if part == "cond":
                    cond_o[layer] = piece
                elif part == "res":
                    res_o[layer] = piece
                else:
                    in_o[layer, part] = piece
                row += high

        when_owner(chunk_id, me_tm, run)

    def drain(chunk_id):
        for stage in range(p.bits):
            stage_copy(chunk_id, stage).wait_send()
        for step in range(1, p.tm):
            when_owner(
                chunk_id, lax.rem(me_tm + step, p.tm), tm_copy(chunk_id, step).wait_send
            )

    lane_iota = lax.broadcasted_iota(jnp.int32, (p.group, LANES), 1)
    row_iota = lax.broadcasted_iota(jnp.int32, (p.group, LANES), 0)
    loads["audio"].wait()
    halo_wait(0)
    halo_lanes = p.pad_rows - rows
    blocks = [jnp.zeros((p.group, LANES), F32) for _ in range(halo_lanes // LANES)]
    lane_ok = [jnp.zeros((p.group, LANES), jnp.int32) for _ in range(halo_lanes // LANES)]
    low_ok = jnp.where(has_low, 1, 0)
    high_ok = jnp.where(has_high, 1, 0)
    for clip in range(p.clips):
        at = clip * 2 * EDGE
        block, lane = at // LANES, at % LANES
        for slot in range(2):
            first = lane + slot * EDGE
            inside = (lane_iota >= first) & (lane_iota < first + EDGE)
            ok = low_ok if slot == 0 else high_ok
            turned = pltpu.roll(s["audio_halo"][slot, clip], (lane + EDGE) % LANES, 1)
            keep = inside & (jnp.broadcast_to(ok, inside.shape) > 0)
            blocks[block] = jnp.where(keep, turned, blocks[block])
            lane_ok[block] = jnp.where(keep, 1, lane_ok[block])
    audio_all = jnp.concatenate(
        [s["audio"][clip] for clip in range(p.clips)] + blocks, axis=1
    )
    main_ok = jnp.ones((p.group, rows), jnp.int32)
    inside_clip = jnp.concatenate([main_ok] + lane_ok, axis=1) > 0
    group_rows = lax.broadcasted_iota(jnp.int32, (p.group, p.pad_rows), 0)
    first8 = jnp.where(group_rows < p.half, audio_all, 0.0)
    s["first"][...] = first8[:, :rows]
    s["second"][...] = pltpu.roll(audio_all, p.half, 0)
    start8 = s["start8"]
    start8[...] = jnp.zeros_like(start8)
    start8[0 : p.half] = start_w[...]
    first_cols = jnp.transpose(first8, (1, 0))
    for block in range(ch // LANES):
        cols = slice(block * LANES, (block + 1) * LANES)
        s["state"][:, cols] = dot(
            first_cols[:all_rows], start8[:, cols], precision=HIGHEST
        )

    for clip in range(p.clips):
        loads[f"mel{clip}"].wait()
    halo_wait(1)
    for clip in range(p.clips):
        low = s["mel_halo"][0, clip].astype(F32)[EDGE:]
        high = s["mel_halo"][1, clip].astype(F32)[:EDGE]
        low = jnp.where(jnp.broadcast_to(low_ok, low.shape) > 0, low, 0.0)
        high = jnp.where(jnp.broadcast_to(high_ok, high.shape) > 0, high, 0.0)
        s["mel"][pl.ds(rows + clip * 2 * EDGE, 2 * EDGE)] = jnp.concatenate(
            [low, high], axis=0
        ).astype(BF16)

    def extended(ref, clip, cols):
        at = rows + clip * 2 * EDGE
        return jnp.concatenate(
            [
                ref[pl.ds(at, EDGE), cols],
                ref[pl.ds(clip * fr, fr), cols],
                ref[pl.ds(at + EDGE, EDGE), cols],
            ],
            axis=0,
        )

    def store_extended(ref, clip, cols, value):
        ref[pl.ds(clip * fr, fr), cols] = value[EDGE : EDGE + fr].astype(BF16)
        ref[pl.ds(rows + clip * 2 * EDGE, 2 * EDGE), cols] = jnp.concatenate(
            [value[:EDGE], value[EDGE + fr :]], axis=0
        ).astype(BF16)

    ext_iota = lax.broadcasted_iota(jnp.int32, (ext, LANES), 0)
    low_row = jnp.broadcast_to(me_tm == 0, (ext, LANES)) & (ext_iota < EDGE)
    high_row = jnp.broadcast_to(me_tm == p.tm - 1, (ext, LANES)) & (
        ext_iota >= EDGE + fr
    )
    outside = low_row | high_row

    def lanes_at(start):
        return pl.ds(pl.multiple_of(start, LANES), LANES)

    def block_at(start):
        return pl.ds(pl.multiple_of(start, BLOCK), BLOCK)

    def spread_state(layer):
        reach = 2**layer

        @pl.loop(0, ch // LANES)
        def _(block):
            for clip in range(p.clips):
                value = extended(s["state"], clip, lanes_at(block * LANES))
                value = jnp.where(outside, 0.0, value)
                for tap in range(p.taps):
                    shift = ((1 - tap) * reach) % ext
                    moved = pltpu.roll(value, shift, 0) if shift else value
                    store_extended(
                        s["taps"], clip, lanes_at(tap * ch + block * LANES), moved
                    )

        mid = p.taps // 2
        s["state_t"][layer] = jnp.transpose(
            s["taps"][0:rows, mid * ch : (mid + 1) * ch], (1, 0)
        )

    def gate(layer):
        @pl.loop(0, n_blocks)
        def _(n):
            pre = []
            for side in range(2):
                cols = block_at(side * ch + n * BLOCK)
                pre.append(
                    dot(s["taps"][...], s["win"][layer, :, cols])
                    + dot(s["mel"][...], s["cond"][layer, :, cols])
                )
            tangent = jnp.tanh(pre[0])
            switch = 0.5 * jnp.tanh(0.5 * pre[1]) + 0.5
            cols = block_at(n * BLOCK)
            s["tangent"][layer, :, cols] = tangent
            s["switch"][layer, :, cols] = switch
            s["gated"][layer, 0:all_rows, cols] = (tangent * switch).astype(BF16)

    def gate_back(layer):
        reach = 2**layer

        @pl.loop(0, ch // LANES)
        def _(block):
            cols = lanes_at(block * LANES)
            for clip in range(p.clips):
                up = extended(s["act"], clip, cols)
                tangent = extended(s["tangent"].at[layer], clip, cols)
                switch = extended(s["switch"].at[layer], clip, cols)
                lift = jnp.where(outside, 0.0, up) * switch
                sides = (
                    lift * (1.0 - tangent * tangent),
                    lift * tangent * (1.0 - switch),
                )
                for side in range(2):
                    for tap in range(p.taps):
                        shift = ((tap - 1) * reach) % ext
                        moved = pltpu.roll(sides[side], shift, 0) if shift else sides[side]
                        store_extended(
                            s["back"], clip,
                            lanes_at(tap * p.wide + side * ch + block * LANES), moved,
                        )

    def put_owned(chunk_id, row, high, cols, value):
        acc = s["grad"][chunk_id]
        for owner in range(p.dp):
            at = tuple((owner >> b) & 1 for b in reversed(range(p.bits)))
            acc[at + (pl.ds(row, high), cols)] = value[
                owner * high : (owner + 1) * high
            ].astype(BF16)

    def weight_grads(chunk_id):
        layer, parts, columns, _ = p.chunks[chunk_id]
        row = 0
        mid = p.taps // 2
        for part in parts:
            high = p.part_rows(part)

            def body(n, part=part, row=row, high=high):
                cols = block_at(n * BLOCK)
                if part == "cond":
                    left = s["mel_t"][...]
                    right = s["back"][0:rows, block_at(mid * p.wide + n * BLOCK)]
                elif part == "res":
                    left = jnp.transpose(s["gated"][layer, 0:rows, :], (1, 0))
                    right = s["join"][0:rows, cols]
                else:
                    left = s["state_t"][layer]
                    right = s["back"][0:rows, block_at(part * p.wide + n * BLOCK)]
                put_owned(chunk_id, row, high, cols, dot(left, right))

            pl.loop(0, columns // BLOCK)(body)
            row += high

    def state_grad(layer, accumulate):
        @pl.loop(0, n_blocks)
        def _(n):
            total = None
            for tap in range(p.taps):
                term = dot(
                    s["back"][:, tap * p.wide : (tap + 1) * p.wide],
                    s["win"][layer, block_at(tap * ch + n * BLOCK), :],
                    ((1,), (1,)),
                )
                total = term if total is None else total + term
            cols = block_at(n * BLOCK)
            if accumulate:
                total = total + s["state"][:, cols]
            s["state"][:, cols] = total

    spread_state(0)
    s["mel_t"][...] = jnp.transpose(s["mel"][0:rows, :], (1, 0))
    loads["win0"].wait()
    loads["cond0"].wait()
    gate(0)
    loads["res"].wait()

    @pl.loop(0, n_blocks)
    def _(n):
        cols = block_at(n * BLOCK)
        s["state"][:, cols] = s["state"][:, cols] + dot(
            s["gated"][0, 0:all_rows, :], s["res"][:, cols]
        )

    spread_state(1)
    loads["last"].wait()
    end_cols = jnp.transpose(end_w[...].astype(F32), (1, 0)).astype(BF16)
    skips = [
        dot(end_cols, s["res"][:, ch:], ((1,), (1,))),
        dot(end_cols, s["last"][...], ((1,), (1,))),
    ]
    for layer in range(p.layers):
        coarse = skips[layer].astype(BF16)
        fine = skips[layer] - coarse.astype(F32)
        s["skip_w"][layer] = jnp.concatenate(
            [coarse.astype(F32), fine], axis=0
        ).astype(BF16)
    loads["win1"].wait()
    loads["cond1"].wait()
    gate(1)

    out = None
    for layer in range(p.layers):
        term = dot(s["skip_w"][layer], s["gated"][layer], ((1,), (1,)))
        term = term[: p.group] + term[p.group :]
        out = term if out is None else out + term
    top = group_rows < p.half
    inside_top = top & inside_clip
    log_scale = jnp.where(inside_top, out, 0.0)
    shift_term = jnp.where(inside_top, pltpu.roll(out, p.half, 0), 0.0)
    growth = jnp.exp(log_scale)
    second = s["second"][...]
    latent = growth * second + shift_term
    scale_inv = 1.0 / (p.clips * p.dp)
    upper = (latent * growth * second - 1.0) * scale_inv
    lower = pltpu.roll(jnp.where(top, latent, 0.0), p.half, 0) * scale_inv
    grad_out = jnp.where(inside_clip, jnp.where(top, upper, lower), 0.0)
    s["scaled"][...] = (jnp.where(top, latent * growth, 0.0) * scale_inv)[:, :rows]
    for clip in range(p.clips):
        latent_o[clip] = latent[0 : p.half, clip * fr : (clip + 1) * fr]
    first = s["first"][...]
    head = (latent * latent)[:, :rows] * 0.5 - log_scale[:, :rows]
    loss = jnp.sum(
        jnp.where(top[:, :rows], head, 0.0) + 0.5 * first * first, keepdims=True
    )
    s["loss"][...] = jnp.broadcast_to(loss * scale_inv, s["loss"].shape)
    grad_twice = jnp.concatenate([grad_out, grad_out], axis=0).astype(BF16)
    grad_b = grad_out.astype(BF16)
    for layer in range(p.layers):
        s["small"][layer * p.group : (layer + 1) * p.group] = dot(
            grad_b[:, :rows], s["gated"][layer, 0:rows, :]
        )
    s["grad_cols"][...] = jnp.transpose(
        jnp.concatenate([grad_out, grad_out], axis=0), (1, 0)
    ).astype(BF16)

    s["act"][...] = dot(s["grad_cols"][0:all_rows], s["skip_w"][1])
    gate_back(1)
    weight_grads(0)
    dp_send(0, 0)
    weight_grads(1)
    dp_send(1, 0)
    dp_send(0, 1)
    state_grad(1, False)
    dp_send(1, 1)

    @pl.loop(0, ch // LANES)
    def _(block):
        cols = lanes_at(block * LANES)
        for clip in range(p.clips):
            value = jnp.where(outside, 0.0, extended(s["state"], clip, cols))
            store_extended(s["join"], clip, cols, value)

    weight_grads(2)
    dp_send(2, 0)

    @pl.loop(0, n_blocks)
    def _(n):
        cols = block_at(n * BLOCK)
        s["act"][:, cols] = dot(
            s["join"][...], s["res"][cols, 0:ch], ((1,), (1,))
        ) + dot(s["grad_cols"][0:all_rows], s["skip_w"][0, :, cols])

    gate_back(0)
    weight_grads(3)
    dp_send(3, 0)
    weight_grads(4)
    dp_send(4, 0)
    late_stages(p, dp_send, tm_send, finish)
    state_grad(0, True)

    small = s["small"]
    lead = 2 * p.group
    start_grad = dot(first, s["state"][0:rows], precision=HIGHEST)
    start_rows = lax.broadcasted_iota(jnp.int32, start_grad.shape, 0)
    small[lead : lead + p.group] = jnp.where(
        start_rows == p.half, jnp.broadcast_to(s["loss"][0:1, 0:1], start_grad.shape),
        start_grad,
    )

    def small_copy(stage):
        return pltpu.make_async_remote_copy(
            small, s["small_recv"].at[stage],
            s["small_send_sem"].at[stage], s["small_recv_sem"].at[stage],
            device_id=partner(stage), device_id_type=MESH,
        )

    def small_tm(step):
        return pltpu.make_async_remote_copy(
            small, s["small_tm"].at[me_tm],
            s["small_tm_send"].at[step - 1], s["small_tm_recv"].at[step - 1],
            device_id=peer(step), device_id_type=MESH,
        )

    def small_step(stage):
        small_copy(stage).wait()
        small[...] = small[...] + s["small_recv"][stage]

    small_copy(0).start()
    first_back = dot(start8[...], s["state"][0:rows], ((1,), (1,)), precision=HIGHEST)
    front = first_back + first * scale_inv
    back_rows = pltpu.roll(s["scaled"][...], p.half, 0)
    audio_grad = jnp.where(group_rows[:, :rows] < p.half, front, back_rows)
    for clip in range(p.clips):
        audio_o[clip] = audio_grad[:, clip * fr : (clip + 1) * fr]
    tail_stages(p, dp_send, tm_send, finish, small_copy, small_step, small_tm)

    s["small_tm"][me_tm] = small[...]
    for step in range(1, p.tm):
        small_tm(step).wait()
    total = s["small_tm"][0]
    for at in range(1, p.tm):
        total += s["small_tm"][at]
    m_first, m_last = total[: p.group], total[p.group : lead]
    loss_o[...] = total[lead + p.half : lead + p.half + 1, 0:1]
    start_o[...] = total[lead : lead + p.half]

    def split(value):
        coarse = value.astype(BF16)
        return coarse, (value - coarse.astype(F32)).astype(BF16)

    end_t = None
    for m, w in ((m_first, s["res"][:, ch:]), (m_last, s["last"][...])):
        for term in split(m):
            part = dot(term, w)
            end_t = part if end_t is None else end_t + part
    end_o[...] = jnp.transpose(end_t, (1, 0))
    end_rows = end_cols
    for m, out_ref in ((m_first, s["res_skip"]), (m_last, last_o)):
        coarse, fine = split(jnp.transpose(m, (1, 0)))
        out_ref[...] = dot(coarse, end_rows) + dot(fine, end_rows)
    res_owners = ch // p.width

    @pl.when(me_tm >= res_owners)
    def _():
        cols = pl.ds(
            pl.multiple_of((me_tm - res_owners) * p.width, LANES), p.width
        )
        at = pl.ds(pl.multiple_of(me_dp * p.own_ch, p.own_ch), p.own_ch)
        res_o[0] = s["res_skip"][at, cols]

    for chunk_id in range(len(p.chunks)):
        finish(chunk_id)

    for chunk_id in range(len(p.chunks)):
        drain(chunk_id)

    @pl.when(has_high)
    def _():
        for copy in to_high:
            copy.wait_send()

    @pl.when(has_low)
    def _():
        for copy in to_low:
            copy.wait_send()


def late_stages(p, dp_send, tm_send, finish):
    for stage in range(2, p.bits):
        dp_send(0, stage)
        dp_send(1, stage)
    for chunk in (2, 3, 4):
        dp_send(chunk, 1)


def tail_stages(p, dp_send, tm_send, finish, small_copy, small_step, small_tm):
    tm_send(0)
    tm_send(1)
    for stage in range(1, p.bits):
        small_step(stage - 1)
        small_copy(stage).start()
    small_step(p.bits - 1)
    for step in range(1, p.tm):
        small_tm(step).start()
    for stage in range(2, p.bits):
        for chunk in (2, 3, 4):
            dp_send(chunk, stage)
    for chunk in (2, 3, 4):
        tm_send(chunk)


def solution(mesh):
    def shards(
        audio, mel_frames, start_weight, input_weight, cond_weight, res_weight,
        last_weight, end_weight,
    ):
        p = Plan(mesh, audio, mel_frames, start_weight, input_weight)
        ch, wide, dp = p.channels, p.wide, p.dp
        vmem, anywhere = pltpu.VMEM, pl.BlockSpec(memory_space=pl.ANY)
        inside = pl.BlockSpec(memory_space=pltpu.VMEM)
        twos = (2,) * p.bits
        heights = [p.chunk_rows(chunk) for chunk in p.chunks]
        widths = [chunk[2] for chunk in p.chunks]
        n_chunks = len(p.chunks)
        sem = pltpu.SemaphoreType.DMA
        scratch = {
            "audio": vmem(audio.shape, F32),
            "audio_halo": vmem((2, p.clips, p.group, LANES), F32),
            "mel": vmem((p.all_rows, p.cond), BF16),
            "mel_halo": vmem((2, p.clips, 2 * EDGE, p.cond), BF16),
            "mel_t": vmem((p.cond, p.rows), BF16),
            "win": vmem((p.layers, p.taps * ch, wide), BF16),
            "cond": vmem((p.layers, p.cond, wide), BF16),
            "res": vmem((ch, wide), BF16),
            "last": vmem((ch, ch), BF16),
            "first": vmem((p.group, p.rows), F32),
            "second": vmem((p.group, p.pad_rows), F32),
            "scaled": vmem((p.group, p.rows), F32),
            "start8": vmem((p.group, ch), F32),
            "loss": vmem((p.group, LANES), F32),
            "state": vmem((p.all_rows, ch), F32),
            "act": vmem((p.all_rows, ch), F32),
            "taps": vmem((p.all_rows, p.taps * ch), BF16),
            "state_t": vmem((p.layers, ch, p.rows), BF16),
            "tangent": vmem((p.layers, p.all_rows, ch), F32),
            "switch": vmem((p.layers, p.all_rows, ch), F32),
            "gated": vmem((p.layers, p.pad_rows, ch), BF16),
            "skip_w": vmem((p.layers, 2 * p.group, ch), BF16),
            "grad_cols": vmem((p.pad_rows, 2 * p.group), BF16),
            "join": vmem((p.all_rows, ch), BF16),
            "back": vmem((p.all_rows, p.taps * wide), BF16),
            "res_skip": vmem((ch, ch), F32),
            "small": vmem((3 * p.group, ch), F32),
            "small_recv": vmem((p.bits, 3 * p.group, ch), F32),
            "small_tm": vmem((p.tm, 3 * p.group, ch), F32),
            "grad": [vmem(twos + (h, w), BF16) for h, w in zip(heights, widths)],
            "recv": [
                [vmem((2,) * (p.bits - 1 - st) + (h, w), BF16) for st in range(p.bits)]
                for h, w in zip(heights, widths)
            ],
            "tm_recv_buf": [vmem((p.tm - 1, h, p.width), BF16) for h in heights],
            "load_sem": sem((3 + p.clips + 2 * p.layers,)),
            "halo_send": sem((2, 2)),
            "halo_recv": sem((2, 2)),
            "dp_send": sem((n_chunks, p.bits)),
            "dp_recv": sem((n_chunks, p.bits)),
            "tm_send": sem((n_chunks, p.tm - 1)),
            "tm_recv": sem((n_chunks, p.tm - 1)),
            "small_send_sem": sem((p.bits,)),
            "small_recv_sem": sem((p.bits,)),
            "small_tm_send": sem((p.tm - 1,)),
            "small_tm_recv": sem((p.tm - 1,)),
        }
        leaves, tree = jax.tree.flatten(scratch)

        def entry(*refs):
            fixed = 8 + 9
            kernel(p, *refs[:fixed], jax.tree.unflatten(tree, refs[fixed:]))

        shape = jax.ShapeDtypeStruct
        outs = pl.pallas_call(
            entry,
            out_shape=[
                shape((p.clips, p.half, p.frames), F32),
                shape(audio.shape, F32),
                shape((1, 1), F32),
                shape((p.layers, p.taps, p.own_ch, p.width), F32),
                shape((p.layers, p.own_cond, p.width), F32),
                shape((p.layers - 1, p.own_ch, p.width), F32),
                shape(last_weight.shape, F32),
                shape(end_weight.shape, F32),
                shape(start_weight.shape, F32),
            ],
            in_specs=[
                anywhere, anywhere, inside, anywhere, anywhere, anywhere, anywhere, inside
            ],
            out_specs=[inside] * 9,
            scratch_shapes=leaves,
            compiler_params=pltpu.CompilerParams(
                collective_id=0, has_side_effects=True,
                vmem_limit_bytes=67_043_328,
            ),
            name="coupling_step",
        )(
            audio,
            mel_frames,
            start_weight,
            input_weight.reshape(p.layers, p.taps * ch, wide),
            cond_weight,
            res_weight.reshape(ch, wide),
            last_weight,
            end_weight,
        )
        outs = list(outs)
        outs[2] = outs[2].reshape(())
        return tuple(outs)

    return jax.shard_map(
        shards,
        mesh=mesh,
        in_specs=(P("dp", None, "tm"), P("dp", "tm", None), P(), P(), P(), P(), P(), P()),
        out_specs=(
            P("dp", None, "tm"),
            P("dp", None, "tm"),
            P(),
            P(None, None, "dp", "tm"),
            P(None, "dp", "tm"),
            P(None, "dp", "tm"),
            P(),
            P(),
            P(),
        ),
        check_vma=False,
    )
```

time: 226 us -> 110 us (0.49)
  Pallas kernels: 0 us -> 93.1 us
  blocking collectives: 67.5 us -> 0 us
  matrix products: 48.9 us -> 0 us
  waiting for transfers between devices: 28.5 us -> 0 us
  starting transfers between devices: 25.3 us -> 0 us
  local copies, waits for them, and re-layouts: 31 us -> 14.2 us
  between operations: 16.4 us -> 2.42 us
  other arithmetic: 7.3 us -> 0 us
    pallas_call x0 -> x1, Pallas kernels: none -> 93.1 us  [shards(): pl.pallas_call(entry, out_shape=[shape((p.clips, p.half, p.frames), F32),...]
    dot_general x34 -> x0, matrix products: 48.9 us -> none  [the longest x6 15.2 us: dilated_back(): jnp.einsum('cto,io->cti', window, weight[tap_index], preferred_element_ty...]
    psum x2 -> x0, blocking collectives: 41.7 us -> none  [shards(): small = lax.psum(lax.psum(small, 'tm'), 'dp')]
    all_gather x2 -> x0, blocking collectives: 25.7 us -> none  [the longest x1 13.9 us: shards(): last_parts = lax.all_gather(clip_sums[-1][grad_rows:], 'tm')]
    reduce_scatter x3 -> x0, waiting for transfers between devices: 25.4 us -> none  [the longest x1 25.4 us: shards(): lax.psum_scatter(by_frame_owner, 'tm', scatter_dimension=0, tiled=True)[0]]
    ppermute x8 -> x0, starting transfers between devices: 25.2 us -> none  [the longest x4 19.7 us: with_halo(): lax.ppermute(lax.slice_in_dim(block, block.shape[dim] - width, None, axis...]
    slice x10 -> x0, local copies, waits for them, and re-layouts: 4.6 us -> none  [the longest x1 1.39 us: shards(): res_sums.append(mine[taken:taken + rows])]
    convert_element_type x2 -> x0, local copies, waits for them, and re-layouts: 4.36 us -> none  [shards(): unfolded(lax.all_gather(last_rows, 'dp', tiled=True)).astype(jnp.float32)]
  transfers between devices with their start and end apart: 11 -> 0, of which waited for: 2 -> 0; matrix products, arithmetic and copies ran while one was open for 21% -> 0% of each run, Pallas kernels for 0% -> 0%
where the time goes in v1:
time: 110 us
  Pallas kernels  93.1 us (85%)
  local copies, waits for them, and re-layouts  14.2 us (13%)
  between operations  2.42 us (2%)
    pallas_call x1, Pallas kernels, shards(): pl.pallas_call(entry, out_shape=[shape((p.clips, p.half, p.frames), F32),...  93.1 us
    unnamed x9, local copies, waits for them, and re-layouts  14.2 us

profile of v1, /device:TPU:0, one launch (start us, length us, event | category | flops | bytes accessed | tf_op | source)
XLA Modules:
  0.0 109.7 jit_solution(581254596864367671)
XLA Ops:
  0.6 1.5 %copy.17.refs_7_ = bf16[512,8]{1,0:T(8,128)(2,1)} copy(bf16[512,8]{0,1:T(8,128)(2,1)} %param.15) | data formatting | bytes 16384 | tf_op args[7]
  2.1 93.1 %coupling_step.1 = (f32[3,4,256]{2,1,0:T(4,128)}, f32[3,8,256]{2,1,0:T(8,128)}, f32[1,1]{1,0:T(1,128)}, f32[2,3,64,256]{3,2,1,0:T(8,128)}, f32[2,80,256]{2,1,0:T...) custom-call(f32[3,8,256]{2,1,0:T(8,128)} %refs_0_.1, ...), custom_call_target="tpu_custom_call" | custom-call | tf_op jit(solution)/shard_map/coupling_step/pallas_call | solution.py:741
  95.2 1.7 %copy.18 = f32[512,8]{0,1:T(8,128)} copy(f32[512,8]{1,0:T(8,128)} %get-tuple-element.34) | data formatting | bytes 32768
  96.9 1.3 %copy.27 = f32[3,4,256]{2,1,0:T(4,128)} copy(f32[3,4,256]{2,1,0:T(4,128)} %get-tuple-element.45) | data formatting | bytes 24576
  98.2 1.3 %copy.28 = f32[3,8,256]{2,1,0:T(8,128)} copy(f32[3,8,256]{2,1,0:T(8,128)} %get-tuple-element.46) | data formatting | bytes 49152
  100.2 1.8 %copy.30 = f32[2,3,64,256]{3,2,1,0:T(8,128)} copy(f32[2,3,64,256]{3,2,1,0:T(8,128)} %get-tuple-element.48) | data formatting | bytes 786432
  101.9 1.6 %copy.31 = f32[2,80,256]{2,1,0:T(8,128)} copy(f32[2,80,256]{2,1,0:T(8,128)} %get-tuple-element.49) | data formatting | bytes 327680
  103.5 1.5 %copy.32 = f32[1,64,256]{2,1,0:T(8,128)} copy(f32[1,64,256]{2,1,0:T(8,128)} %get-tuple-element.50) | data formatting | bytes 131072
  105.0 2.3 %copy.33 = f32[512,512]{1,0:T(8,128)} copy(f32[512,512]{1,0:T(8,128)} %get-tuple-element.51) | data formatting | bytes 2097152
  107.3 1.3 %copy.34 = f32[4,512]{1,0:T(4,128)} copy(f32[4,512]{1,0:T(4,128)} %get-tuple-element.53) | data formatting | bytes 16384

commit v2 on v1

v2 whole, which is shorter than its diff:
```python
import itertools
import types

import jax
import jax.numpy as jnp
from jax import lax
from jax.experimental import pallas as pl
from jax.experimental.pallas import tpu as pltpu
from jax.sharding import PartitionSpec as P

F32 = jnp.float32
BF16 = jnp.bfloat16
HIGHEST = lax.Precision.HIGHEST
MESH = pl.DeviceIdType.MESH


EDGE = 8
BLOCK = 256
LANES = 128


def dot(a, b, dims=((1,), (0,)), precision=None):
    return lax.dot_general(
        a, b, (dims, ((), ())), precision=precision, preferred_element_type=F32
    )


def round_up(value, unit):
    return -(-value // unit) * unit


class Plan:
    def __init__(self, mesh, audio, mel, start_weight, input_weight):
        self.dp, self.tm = mesh.shape["dp"], mesh.shape["tm"]
        self.bits = self.dp.bit_length() - 1
        self.clips, self.group, self.frames = audio.shape
        self.half = self.group // 2
        self.cond = mel.shape[2]
        self.channels = start_weight.shape[1]
        self.layers, self.taps = input_weight.shape[:2]
        self.wide = 2 * self.channels
        self.rows = self.clips * self.frames
        self.all_rows = self.rows + self.clips * 2 * EDGE
        self.pad_rows = round_up(self.all_rows, LANES)
        self.own_ch = self.channels // self.dp
        self.own_cond = self.cond // self.dp
        self.width = self.wide // self.tm
        order = list(range(self.bits))
        self.first = order
        self.second = order[:1] + order[1:][::-1]
        tap_pair = tuple(range(self.taps - 1))
        rest = (self.taps - 1, "cond")
        self.chunks = [
            (1, tap_pair, self.wide, self.first),
            (1, rest, self.wide, self.second),
            (0, ("res",), self.channels, self.second),
            (0, tap_pair, self.wide, self.first),
            (0, rest, self.wide, self.second),
        ]

    def part_rows(self, part):
        return self.own_cond if part == "cond" else self.own_ch

    def chunk_rows(self, chunk):
        return round_up(sum(self.part_rows(part) for part in chunk[1]), 16)


def kernel(plan, *refs):
    p = plan
    n_in, n_out = 8, 7
    (audio_h, mel_h, start_w, win_h, cond_h, res_h, last_h, end_w) = refs[:n_in]
    latent_o, audio_o, in_o, cond_o, res_o, small_o, end_o = refs[n_in : n_in + n_out]
    s = refs[n_in + n_out]
    me_dp, me_tm = lax.axis_index("dp"), lax.axis_index("tm")
    bit_of = [(me_dp // 2**b) % 2 for b in range(p.bits)]
    ch, rows, all_rows, fr = p.channels, p.rows, p.all_rows, p.frames
    ext = fr + 2 * EDGE
    n_blocks = ch // BLOCK

    def partner(b):
        return {"dp": me_dp + (2**b) * (1 - 2 * bit_of[b]), "tm": me_tm}

    def peer(step):
        return {"dp": me_dp, "tm": lax.rem(me_tm + step, p.tm)}

    def load(src, dst, index):
        copy = pltpu.make_async_copy(src, dst, s.load_sem.at[index])
        copy.start()
        return copy

    audio_load = load(audio_h, s.audio, 0)
    mel_loads = [
        load(mel_h.at[clip], s.mel.at[pl.ds(clip * fr, fr)], 1 + clip)
        for clip in range(p.clips)
    ]
    base = 1 + p.clips
    weight_loads = []
    for layer in range(p.layers):
        at = base + 2 * layer
        weight_loads.append(
            [
                load(win_h.at[layer], s.win.at[layer], at),
                load(cond_h.at[layer], s.cond.at[layer], at + 1),
            ]
        )
        if layer == 0:
            res_load = load(res_h, s.res, base + 2 * p.layers)
            last_load = load(last_h, s.last, base + 2 * p.layers + 1)

    barrier = pltpu.get_barrier_semaphore()
    for b in range(p.bits):
        pl.semaphore_signal(barrier, 1, device_id=partner(b), device_id_type=MESH)
    for step in range(1, p.tm):
        pl.semaphore_signal(barrier, 1, device_id=peer(step), device_id_type=MESH)
    pl.semaphore_wait(barrier, p.bits + p.tm - 1)

    has_low, has_high = me_tm > 0, me_tm < p.tm - 1

    def halo_copies(slot):
        device = {"dp": me_dp, "tm": me_tm + 1 if slot == 0 else me_tm - 1}
        mel_at = fr - 2 * EDGE if slot == 0 else 0
        audio_at = fr - LANES if slot == 0 else 0
        return [
            pltpu.make_async_remote_copy(
                audio_h.at[:, :, pl.ds(audio_at, LANES)],
                s.audio_halo.at[slot],
                s.halo_send.at[slot, 0], s.halo_recv.at[slot, 0],
                device_id=device, device_id_type=MESH,
            ),
            pltpu.make_async_remote_copy(
                mel_h.at[:, pl.ds(mel_at, 2 * EDGE)],
                s.mel_halo.at[slot],
                s.halo_send.at[slot, 1], s.halo_recv.at[slot, 1],
                device_id=device, device_id_type=MESH,
            ),
        ]

    to_high, to_low = halo_copies(0), halo_copies(1)

    @pl.when(has_high)
    def _():
        for copy in to_high:
            copy.start()

    @pl.when(has_low)
    def _():
        for copy in to_low:
            copy.start()

    def halo_wait(index):
        @pl.when(has_low)
        def _():
            to_high[index].wait_recv()

        @pl.when(has_high)
        def _():
            to_low[index].wait_recv()

    def free_bits(order, stage):
        done = set(order[:stage])
        return [b for b in reversed(range(p.bits)) if b not in done]

    def g_index(values):
        return tuple(values[b] for b in reversed(range(p.bits)))

    def g_blocks(chunk_id, stage, other):
        order = p.chunks[chunk_id][3]
        bit = order[stage]
        free = free_bits(order, stage + 1)
        for combo in itertools.product((0, 1), repeat=len(free)):
            values = {b: bit_of[b] for b in order[:stage]}
            values[bit] = 1 - bit_of[bit] if other else bit_of[bit]
            values.update(zip(free, combo))
            yield values

    def recv_index(order, stage, values):
        return tuple(values[b] for b in free_bits(order, stage + 1))

    def add_block(chunk_id, stages, values):
        order = p.chunks[chunk_id][3]
        acc = s.grad[chunk_id]
        at = g_index(values)
        height = acc.shape[-2]

        @pl.loop(0, height // 16)
        def _(r):
            where = (pl.ds(pl.multiple_of(r * 16, 16), 16),)
            total = acc[at + where].astype(F32)
            for stage in range(stages):
                buf = s.recv[chunk_id][stage]
                total += buf[recv_index(order, stage, values) + where].astype(F32)
            acc[at + where] = total.astype(BF16)

    def stage_copy(chunk_id, stage):
        order = p.chunks[chunk_id][3]
        bit = order[stage]
        values = {b: slice(None) for b in range(p.bits)}
        values.update({b: bit_of[b] for b in order[:stage]})
        values[bit] = 1 - bit_of[bit]
        return pltpu.make_async_remote_copy(
            s.grad[chunk_id].at[g_index(values)],
            s.recv[chunk_id][stage],
            s.dp_send.at[chunk_id, stage], s.dp_recv.at[chunk_id, stage],
            device_id=partner(bit), device_id_type=MESH,
        )

    def dp_send(chunk_id, stage):
        if stage:
            stage_copy(chunk_id, stage - 1).wait_recv()
            for values in g_blocks(chunk_id, stage, True):
                add_block(chunk_id, stage, values)
        stage_copy(chunk_id, stage).start()

    def owners(chunk_id):
        return p.chunks[chunk_id][2] // p.width

    def tm_copy(chunk_id, step):
        target = lax.rem(me_tm + step, p.tm)
        at = g_index({b: bit_of[b] for b in range(p.bits)})
        place = lax.rem(target, owners(chunk_id))
        cols = pl.ds(pl.multiple_of(place * p.width, LANES), p.width)
        return pltpu.make_async_remote_copy(
            s.grad[chunk_id].at[at + (slice(None), cols)],
            s.tm_recv_buf[chunk_id].at[step - 1],
            s.tm_send.at[chunk_id, step - 1], s.tm_recv.at[chunk_id, step - 1],
            device_id={"dp": me_dp, "tm": target}, device_id_type=MESH,
        )

    def when_owner(chunk_id, position, run):
        if owners(chunk_id) == p.tm:
            run()
        else:
            pl.when(position < owners(chunk_id))(run)

    def tm_send(chunk_id):
        stage_copy(chunk_id, p.bits - 1).wait_recv()
        add_block(chunk_id, p.bits, {b: bit_of[b] for b in range(p.bits)})
        for step in range(1, p.tm):
            when_owner(
                chunk_id, lax.rem(me_tm + step, p.tm), tm_copy(chunk_id, step).start
            )

    def finish(chunk_id):
        layer, parts, _, _ = p.chunks[chunk_id]
        at = g_index({b: bit_of[b] for b in range(p.bits)})

        def run():
            for step in range(1, p.tm):
                tm_copy(chunk_id, step).wait_recv()
            cols = pl.ds(pl.multiple_of(me_tm * p.width, LANES), p.width)
            total = s.grad[chunk_id][at + (slice(None), cols)].astype(F32)
            for step in range(1, p.tm):
                total += s.tm_recv_buf[chunk_id][step - 1].astype(F32)
            row = 0
            for part in parts:
                high = p.part_rows(part)
                piece = total[row : row + high]
                if part == "cond":
                    cond_o[layer] = piece
                elif part == "res":
                    res_o[layer] = piece
                else:
                    in_o[layer, part] = piece
                row += high

        when_owner(chunk_id, me_tm, run)

    def drain(chunk_id):
        for stage in range(p.bits):
            stage_copy(chunk_id, stage).wait_send()
        for step in range(1, p.tm):
            when_owner(
                chunk_id, lax.rem(me_tm + step, p.tm), tm_copy(chunk_id, step).wait_send
            )

    lane_iota = lax.broadcasted_iota(jnp.int32, (p.group, LANES), 1)
    row_iota = lax.broadcasted_iota(jnp.int32, (p.group, LANES), 0)
    audio_load.wait()
    halo_wait(0)
    halo_lanes = p.pad_rows - rows
    blocks = [jnp.zeros((p.group, LANES), F32) for _ in range(halo_lanes // LANES)]
    lane_ok = [jnp.zeros((p.group, LANES), jnp.int32) for _ in range(halo_lanes // LANES)]
    low_ok = jnp.where(has_low, 1, 0)
    high_ok = jnp.where(has_high, 1, 0)
    for clip in range(p.clips):
        at = clip * 2 * EDGE
        block, lane = at // LANES, at % LANES
        for slot in range(2):
            first = lane + slot * EDGE
            inside = (lane_iota >= first) & (lane_iota < first + EDGE)
            ok = low_ok if slot == 0 else high_ok
            turned = pltpu.roll(s.audio_halo[slot, clip], (lane + EDGE) % LANES, 1)
            keep = inside & (jnp.broadcast_to(ok, inside.shape) > 0)
            blocks[block] = jnp.where(keep, turned, blocks[block])
            lane_ok[block] = jnp.where(keep, 1, lane_ok[block])
    audio_all = jnp.concatenate(
        [s.audio[clip] for clip in range(p.clips)] + blocks, axis=1
    )
    main_ok = jnp.ones((p.group, rows), jnp.int32)
    inside_clip = jnp.concatenate([main_ok] + lane_ok, axis=1) > 0
    group_rows = lax.broadcasted_iota(jnp.int32, (p.group, p.pad_rows), 0)
    first8 = jnp.where(group_rows < p.half, audio_all, 0.0)
    s.first[...] = first8[:, :rows]
    s.second[...] = pltpu.roll(audio_all, p.half, 0)
    start8 = s.start8
    start8[...] = jnp.zeros_like(start8)
    start8[0 : p.half] = start_w[...]
    first_cols = jnp.transpose(first8, (1, 0))
    for block in range(ch // LANES):
        cols = slice(block * LANES, (block + 1) * LANES)
        s.state[:, cols] = dot(
            first_cols[:all_rows], start8[:, cols], precision=HIGHEST
        )

    for clip in range(p.clips):
        mel_loads[clip].wait()
    halo_wait(1)
    for clip in range(p.clips):
        low = s.mel_halo[0, clip].astype(F32)[EDGE:]
        high = s.mel_halo[1, clip].astype(F32)[:EDGE]
        low = jnp.where(jnp.broadcast_to(low_ok, low.shape) > 0, low, 0.0)
        high = jnp.where(jnp.broadcast_to(high_ok, high.shape) > 0, high, 0.0)
        s.mel[pl.ds(rows + clip * 2 * EDGE, 2 * EDGE)] = jnp.concatenate(
            [low, high], axis=0
        ).astype(BF16)

    def extended(ref, clip, cols):
        at = rows + clip * 2 * EDGE
        return jnp.concatenate(
            [
                ref[pl.ds(at, EDGE), cols],
                ref[pl.ds(clip * fr, fr), cols],
                ref[pl.ds(at + EDGE, EDGE), cols],
            ],
            axis=0,
        )

    def store_extended(ref, clip, cols, value):
        ref[pl.ds(clip * fr, fr), cols] = value[EDGE : EDGE + fr].astype(BF16)
        ref[pl.ds(rows + clip * 2 * EDGE, 2 * EDGE), cols] = jnp.concatenate(
            [value[:EDGE], value[EDGE + fr :]], axis=0
        ).astype(BF16)

    ext_iota = lax.broadcasted_iota(jnp.int32, (ext, LANES), 0)
    low_row = jnp.broadcast_to(me_tm == 0, (ext, LANES)) & (ext_iota < EDGE)
    high_row = jnp.broadcast_to(me_tm == p.tm - 1, (ext, LANES)) & (
        ext_iota >= EDGE + fr
    )
    outside = low_row | high_row

    def lanes_at(start):
        return pl.ds(pl.multiple_of(start, LANES), LANES)

    def block_at(start):
        return pl.ds(pl.multiple_of(start, BLOCK), BLOCK)

    def spread_state(layer):
        reach = 2**layer

        @pl.loop(0, ch // LANES)
        def _(block):
            for clip in range(p.clips):
                value = extended(s.state, clip, lanes_at(block * LANES))
                value = jnp.where(outside, 0.0, value)
                for tap in range(p.taps):
                    shift = ((1 - tap) * reach) % ext
                    moved = pltpu.roll(value, shift, 0) if shift else value
                    store_extended(
                        s.taps, clip, lanes_at(tap * ch + block * LANES), moved
                    )

        mid = p.taps // 2
        s.state_t[layer] = jnp.transpose(
            s.taps[0:rows, mid * ch : (mid + 1) * ch], (1, 0)
        )

    def gate(layer):
        @pl.loop(0, n_blocks)
        def _(n):
            pre = []
            for side in range(2):
                cols = block_at(side * ch + n * BLOCK)
                pre.append(
                    dot(s.taps[...], s.win[layer, :, cols])
                    + dot(s.mel[...], s.cond[layer, :, cols])
                )
            tangent = jnp.tanh(pre[0])
            switch = 0.5 * jnp.tanh(0.5 * pre[1]) + 0.5
            cols = block_at(n * BLOCK)
            s.tangent[layer, :, cols] = tangent
            s.switch[layer, :, cols] = switch
            s.gated[layer, 0:all_rows, cols] = (tangent * switch).astype(BF16)

    def gate_back(layer):
        reach = 2**layer

        @pl.loop(0, ch // LANES)
        def _(block):
            cols = lanes_at(block * LANES)
            for clip in range(p.clips):
                up = extended(s.act, clip, cols)
                tangent = extended(s.tangent.at[layer], clip, cols)
                switch = extended(s.switch.at[layer], clip, cols)
                lift = jnp.where(outside, 0.0, up) * switch
                sides = (
                    lift * (1.0 - tangent * tangent),
                    lift * tangent * (1.0 - switch),
                )
                for side in range(2):
                    for tap in range(p.taps):
                        shift = ((tap - 1) * reach) % ext
                        moved = pltpu.roll(sides[side], shift, 0) if shift else sides[side]
                        store_extended(
                            s.back, clip,
                            lanes_at(tap * p.wide + side * ch + block * LANES), moved,
                        )

    def put_owned(chunk_id, row, high, cols, value):
        acc = s.grad[chunk_id]
        for owner in range(p.dp):
            at = tuple((owner >> b) & 1 for b in reversed(range(p.bits)))
            acc[at + (pl.ds(row, high), cols)] = value[
                owner * high : (owner + 1) * high
            ].astype(BF16)

    def weight_grads(chunk_id):
        layer, parts, columns, _ = p.chunks[chunk_id]
        row = 0
        mid = p.taps // 2
        for part in parts:
            high = p.part_rows(part)

            def body(n, part=part, row=row, high=high):
                cols = block_at(n * BLOCK)
                if part == "cond":
                    left = s.mel_t[...]
                    right = s.back[0:rows, block_at(mid * p.wide + n * BLOCK)]
                elif part == "res":
                    left = jnp.transpose(s.gated[layer, 0:rows, :], (1, 0))
                    right = s.join[0:rows, cols]
                else:
                    left = s.state_t[layer]
                    right = s.back[0:rows, block_at(part * p.wide + n * BLOCK)]
                put_owned(chunk_id, row, high, cols, dot(left, right))

            pl.loop(0, columns // BLOCK)(body)
            row += high

    def state_grad(layer, accumulate):
        @pl.loop(0, n_blocks)
        def _(n):
            total = None
            for tap in range(p.taps):
                term = dot(
                    s.back[:, tap * p.wide : (tap + 1) * p.wide],
                    s.win[layer, block_at(tap * ch + n * BLOCK), :],
                    ((1,), (1,)),
                )
                total = term if total is None else total + term
            cols = block_at(n * BLOCK)
            if accumulate:
                total = total + s.state[:, cols]
            s.state[:, cols] = total

    spread_state(0)
    s.mel_t[...] = jnp.transpose(s.mel[0:rows, :], (1, 0))
    for copy in weight_loads[0]:
        copy.wait()
    gate(0)
    res_load.wait()

    @pl.loop(0, n_blocks)
    def _(n):
        cols = block_at(n * BLOCK)
        s.state[:, cols] = s.state[:, cols] + dot(
            s.gated[0, 0:all_rows, :], s.res[:, cols]
        )

    spread_state(1)
    last_load.wait()
    end_cols = end_w[...]
    skips = [
        dot(end_cols, s.res[:, ch:], ((1,), (1,))),
        dot(end_cols, s.last[...], ((1,), (1,))),
    ]
    for layer in range(p.layers):
        coarse = skips[layer].astype(BF16)
        fine = skips[layer] - coarse.astype(F32)
        s.skip_w[layer] = jnp.concatenate(
            [coarse.astype(F32), fine], axis=0
        ).astype(BF16)
    for copy in weight_loads[1]:
        copy.wait()
    gate(1)

    out = None
    for layer in range(p.layers):
        term = dot(s.skip_w[layer], s.gated[layer], ((1,), (1,)))
        term = term[: p.group] + term[p.group :]
        out = term if out is None else out + term
    top = group_rows < p.half
    inside_top = top & inside_clip
    log_scale = jnp.where(inside_top, out, 0.0)
    shift_term = jnp.where(inside_top, pltpu.roll(out, p.half, 0), 0.0)
    growth = jnp.exp(log_scale)
    second = s.second[...]
    latent = growth * second + shift_term
    scale_inv = 1.0 / (p.clips * p.dp)
    upper = (latent * growth * second - 1.0) * scale_inv
    lower = pltpu.roll(jnp.where(top, latent, 0.0), p.half, 0) * scale_inv
    grad_out = jnp.where(inside_clip, jnp.where(top, upper, lower), 0.0)
    s.scaled[...] = (jnp.where(top, latent * growth, 0.0) * scale_inv)[:, :rows]
    for clip in range(p.clips):
        latent_o[clip] = latent[0 : p.half, clip * fr : (clip + 1) * fr]
    first = s.first[...]
    head = (latent * latent)[:, :rows] * 0.5 - log_scale[:, :rows]
    loss = jnp.sum(
        jnp.where(top[:, :rows], head, 0.0) + 0.5 * first * first, keepdims=True
    )
    s.loss[...] = jnp.broadcast_to(loss * scale_inv, s.loss.shape)
    grad_twice = jnp.concatenate([grad_out, grad_out], axis=0).astype(BF16)
    grad_b = grad_out.astype(BF16)
    for layer in range(p.layers):
        s.small[layer * p.group : (layer + 1) * p.group] = dot(
            grad_b[:, :rows], s.gated[layer, 0:rows, :]
        )
    s.grad_cols[...] = jnp.transpose(
        jnp.concatenate([grad_out, grad_out], axis=0), (1, 0)
    ).astype(BF16)

    s.act[...] = dot(s.grad_cols[0:all_rows], s.skip_w[1])
    gate_back(1)
    weight_grads(0)
    dp_send(0, 0)
    weight_grads(1)
    dp_send(1, 0)
    dp_send(0, 1)
    state_grad(1, False)
    dp_send(1, 1)

    @pl.loop(0, ch // LANES)
    def _(block):
        cols = lanes_at(block * LANES)
        for clip in range(p.clips):
            value = jnp.where(outside, 0.0, extended(s.state, clip, cols))
            store_extended(s.join, clip, cols, value)

    weight_grads(2)
    dp_send(2, 0)

    @pl.loop(0, n_blocks)
    def _(n):
        cols = block_at(n * BLOCK)
        s.act[:, cols] = dot(
            s.join[...], s.res[cols, 0:ch], ((1,), (1,))
        ) + dot(s.grad_cols[0:all_rows], s.skip_w[0, :, cols])

    gate_back(0)
    weight_grads(3)
    dp_send(3, 0)
    weight_grads(4)
    dp_send(4, 0)
    late_stages(p, dp_send, tm_send, finish)
    state_grad(0, True)

    small = s.small
    lead = 2 * p.group
    start_grad = dot(first, s.state[0:rows], precision=HIGHEST)
    start_rows = lax.broadcasted_iota(jnp.int32, start_grad.shape, 0)
    small[lead : lead + p.group] = jnp.where(
        start_rows == p.half, jnp.broadcast_to(s.loss[0:1, 0:1], start_grad.shape),
        start_grad,
    )

    def small_copy(stage):
        return pltpu.make_async_remote_copy(
            small, s.small_recv.at[stage],
            s.small_send_sem.at[stage], s.small_recv_sem.at[stage],
            device_id=partner(stage), device_id_type=MESH,
        )

    def small_tm(step):
        return pltpu.make_async_remote_copy(
            small, s.small_tm.at[me_tm],
            s.small_tm_send.at[step - 1], s.small_tm_recv.at[step - 1],
            device_id=peer(step), device_id_type=MESH,
        )

    def small_step(stage):
        small_copy(stage).wait()
        small[...] = small[...] + s.small_recv[stage]

    small_copy(0).start()
    first_back = dot(start8[...], s.state[0:rows], ((1,), (1,)), precision=HIGHEST)
    front = first_back + first * scale_inv
    back_rows = pltpu.roll(s.scaled[...], p.half, 0)
    audio_grad = jnp.where(group_rows[:, :rows] < p.half, front, back_rows)
    for clip in range(p.clips):
        audio_o[clip] = audio_grad[:, clip * fr : (clip + 1) * fr]
    tail_stages(p, dp_send, tm_send, finish, small_copy, small_step, small_tm)

    s.small_tm[me_tm] = small[...]
    for step in range(1, p.tm):
        small_tm(step).wait()
    total = s.small_tm[0]
    for at in range(1, p.tm):
        total += s.small_tm[at]
    m_first, m_last = total[: p.group], total[p.group : lead]
    small_o[...] = total
    end_t = None
    for m, w in ((m_first, s.res[:, ch:]), (m_last, s.last[...])):
        for term in split(m):
            part = dot(term, w)
            end_t = part if end_t is None else end_t + part
    end_o[...] = end_t

    for chunk_id in range(len(p.chunks)):
        finish(chunk_id)

    for chunk_id in range(len(p.chunks)):
        drain(chunk_id)

    @pl.when(has_high)
    def _():
        for copy in to_high:
            copy.wait_send()

    @pl.when(has_low)
    def _():
        for copy in to_low:
            copy.wait_send()


def split(value):
    coarse = value.astype(BF16)
    return coarse, (value - coarse.astype(F32)).astype(BF16)


def outputs_kernel(plan, *refs):
    p = plan
    (latent_i, audio_i, in_i, cond_i, res_i, small_i, end_i, end_w) = refs[:8]
    (
        latent_o, audio_o, loss_o, in_o, cond_o, res_o, last_o, end_o, start_o, skip
    ) = refs[8:]
    me_dp, me_tm = lax.axis_index("dp"), lax.axis_index("tm")
    lead = 2 * p.group
    for source, target in (
        (latent_i, latent_o), (audio_i, audio_o), (in_i, in_o), (cond_i, cond_o),
        (end_i, end_o),
    ):
        target[...] = source[...]
    loss_o[...] = small_i[lead + p.half : lead + p.half + 1, 0:1]
    start_o[...] = small_i[lead : lead + p.half]
    end_rows = end_w[...]
    for at, out_ref in ((0, skip), (p.group, last_o)):
        m_cols = jnp.transpose(small_i[at : at + p.group], (1, 0))
        coarse, fine = split(m_cols)
        out_ref[...] = dot(coarse, end_rows) + dot(fine, end_rows)
    res_owners = p.channels // p.width

    @pl.when(me_tm < res_owners)
    def _():
        res_o[...] = res_i[...]

    @pl.when(me_tm >= res_owners)
    def _():
        cols = pl.ds(pl.multiple_of((me_tm - res_owners) * p.width, LANES), p.width)
        at = pl.ds(pl.multiple_of(me_dp * p.own_ch, p.own_ch), p.own_ch)
        res_o[0] = skip[at, cols]


def late_stages(p, dp_send, tm_send, finish):
    for stage in range(2, p.bits):
        dp_send(0, stage)
        dp_send(1, stage)
    for chunk in (2, 3, 4):
        dp_send(chunk, 1)


def tail_stages(p, dp_send, tm_send, finish, small_copy, small_step, small_tm):
    tm_send(0)
    tm_send(1)
    for stage in range(1, p.bits):
        small_step(stage - 1)
        small_copy(stage).start()
    small_step(p.bits - 1)
    for step in range(1, p.tm):
        small_tm(step).start()
    for stage in range(2, p.bits):
        for chunk in (2, 3, 4):
            dp_send(chunk, stage)
    for chunk in (2, 3, 4):
        tm_send(chunk)


def solution(mesh):
    def shards(
        audio, mel_frames, start_weight, input_weight, cond_weight, res_weight,
        last_weight, end_weight,
    ):
        p = Plan(mesh, audio, mel_frames, start_weight, input_weight)
        ch, wide, dp = p.channels, p.wide, p.dp
        vmem, anywhere = pltpu.VMEM, pl.BlockSpec(memory_space=pl.ANY)
        inside = pl.BlockSpec(memory_space=pltpu.VMEM)
        twos = (2,) * p.bits
        heights = [p.chunk_rows(chunk) for chunk in p.chunks]
        widths = [chunk[2] for chunk in p.chunks]
        n_chunks = len(p.chunks)
        sem = pltpu.SemaphoreType.DMA
        scratch = dict(
            audio=vmem(audio.shape, F32),
            audio_halo=vmem((2, p.clips, p.group, LANES), F32),
            mel=vmem((p.all_rows, p.cond), BF16),
            mel_halo=vmem((2, p.clips, 2 * EDGE, p.cond), BF16),
            mel_t=vmem((p.cond, p.rows), BF16),
            win=vmem((p.layers, p.taps * ch, wide), BF16),
            cond=vmem((p.layers, p.cond, wide), BF16),
            res=vmem((ch, wide), BF16),
            last=vmem((ch, ch), BF16),
            first=vmem((p.group, p.rows), F32),
            second=vmem((p.group, p.pad_rows), F32),
            scaled=vmem((p.group, p.rows), F32),
            start8=vmem((p.group, ch), F32),
            loss=vmem((p.group, LANES), F32),
            state=vmem((p.all_rows, ch), F32),
            act=vmem((p.all_rows, ch), F32),
            taps=vmem((p.all_rows, p.taps * ch), BF16),
            state_t=vmem((p.layers, ch, p.rows), BF16),
            tangent=vmem((p.layers, p.all_rows, ch), F32),
            switch=vmem((p.layers, p.all_rows, ch), F32),
            gated=vmem((p.layers, p.pad_rows, ch), BF16),
            skip_w=vmem((p.layers, 2 * p.group, ch), BF16),
            grad_cols=vmem((p.pad_rows, 2 * p.group), BF16),
            join=vmem((p.all_rows, ch), BF16),
            back=vmem((p.all_rows, p.taps * wide), BF16),
            small=vmem((3 * p.group, ch), F32),
            small_recv=vmem((p.bits, 3 * p.group, ch), F32),
            small_tm=vmem((p.tm, 3 * p.group, ch), F32),
            grad=[vmem(twos + (h, w), BF16) for h, w in zip(heights, widths)],
            recv=[
                [vmem((2,) * (p.bits - 1 - st) + (h, w), BF16) for st in range(p.bits)]
                for h, w in zip(heights, widths)
            ],
            tm_recv_buf=[vmem((p.tm - 1, h, p.width), BF16) for h in heights],
            load_sem=sem((3 + p.clips + 2 * p.layers,)),
            halo_send=sem((2, 2)),
            halo_recv=sem((2, 2)),
            dp_send=sem((n_chunks, p.bits)),
            dp_recv=sem((n_chunks, p.bits)),
            tm_send=sem((n_chunks, p.tm - 1)),
            tm_recv=sem((n_chunks, p.tm - 1)),
            small_send_sem=sem((p.bits,)),
            small_recv_sem=sem((p.bits,)),
            small_tm_send=sem((p.tm - 1,)),
            small_tm_recv=sem((p.tm - 1,)),
        )
        leaves, tree = jax.tree.flatten(scratch)

        def entry(*refs):
            fixed = 8 + 7
            names = types.SimpleNamespace(**jax.tree.unflatten(tree, refs[fixed:]))
            kernel(p, *refs[:fixed], names)

        shape = jax.ShapeDtypeStruct
        latent = shape((p.clips, p.half, p.frames), F32)
        audio_grad = shape(audio.shape, F32)
        in_grad = shape((p.layers, p.taps, p.own_ch, p.width), F32)
        cond_grad = shape((p.layers, p.own_cond, p.width), F32)
        res_grad = shape((p.layers - 1, p.own_ch, p.width), F32)
        end_grad = shape((p.group, ch), F32)
        end_t = end_weight.T
        held = pl.pallas_call(
            entry,
            out_shape=[
                latent, audio_grad, in_grad, cond_grad, res_grad,
                shape((3 * p.group, ch), F32), end_grad,
            ],
            in_specs=[
                anywhere, anywhere, inside, anywhere, anywhere, anywhere, anywhere, inside
            ],
            out_specs=[inside] * 7,
            scratch_shapes=leaves,
            compiler_params=pltpu.CompilerParams(
                collective_id=0, has_side_effects=True,
                vmem_limit_bytes=67_043_328,
            ),
            name="coupling_step",
        )(
            audio,
            mel_frames,
            start_weight,
            input_weight.reshape(p.layers, p.taps * ch, wide),
            cond_weight,
            res_weight.reshape(ch, wide),
            last_weight,
            end_t,
        )
        outs = pl.pallas_call(
            lambda *refs: outputs_kernel(p, *refs),
            out_shape=[
                latent, audio_grad, shape((1, 1), F32), in_grad, cond_grad, res_grad,
                shape(last_weight.shape, F32), end_grad, shape(start_weight.shape, F32),
            ],
            in_specs=[inside] * 8,
            out_specs=[inside] * 9,
            scratch_shapes=[vmem((ch, ch), F32)],
            name="coupling_outputs",
        )(*held, end_t)
        outs = list(outs)
        outs[2] = outs[2].reshape(())
        outs[7] = outs[7].T
        return tuple(outs)

    return jax.shard_map(
        shards,
        mesh=mesh,
        in_specs=(P("dp", None, "tm"), P("dp", "tm", None), P(), P(), P(), P(), P(), P()),
        out_specs=(
            P("dp", None, "tm"),
            P("dp", None, "tm"),
            P(),
            P(None, None, "dp", "tm"),
            P(None, "dp", "tm"),
            P(None, "dp", "tm"),
            P(),
            P(),
            P(),
        ),
        check_vma=False,
    )
```

time: 110 us -> 96.4 us (0.88)
  local copies, waits for them, and re-layouts: 14.2 us -> 0 us
  Pallas kernels: 93.1 us -> 95.5 us
  between operations: 2.42 us -> 0.65 us
    unnamed x9 -> x0, local copies, waits for them, and re-layouts: 14.2 us -> none
    pallas_call x1 -> x2, Pallas kernels: 93.1 us -> 95.5 us  [the longest x1 92.4 us: shards(): pl.pallas_call(entry, out_shape=[latent, audio_grad, in_grad, cond_grad,...]
where the time goes in v2:
time: 96.4 us; the launch traced here: 96.2 us
  Pallas kernels  95.5 us (99%)
    pallas_call x1, Pallas kernels, shards(): pl.pallas_call(entry, out_shape=[latent, audio_grad, in_grad, cond_grad,...  92.4 us
    pallas_call x1, Pallas kernels, shards(): pl.pallas_call(lambda *refs: outputs_kernel(p, *refs), out_shape=[latent,...  3.14 us

profile of v2, /device:TPU:0, one launch (start us, length us, event | category | flops | bytes accessed | tf_op | source)
XLA Modules:
  0.0 96.2 jit_solution(17913595135709259)
XLA Ops:
  0.6 92.4 %coupling_step.1 = (f32[3,4,256]{2,1,0:T(4,128)}, f32[3,8,256]{2,1,0:T(8,128)}, f32[2,3,64,256]{3,2,1,0:T(8,128)}, f32[2,80,256]{2,1,0:T(8,128)}, f32[1,64,256]{...) custom-call(f32[3,8,256]{2,1,0:T(8,128)} %refs_0_.1, bf16[3,256,640]{2,1,0:T(8,128)(2,1)} %refs_1_.1, ...), custom_call_target="tpu_custom_call" | custom-call | tf_op jit(solution)/shard_map/coupling_step/pallas_call | solution.py:772
  93.0 3.1 %coupling_outputs.1 = (f32[3,4,256]{2,1,0:T(4,128)}, f32[3,8,256]{2,1,0:T(8,128)}, f32[1,1]{1,0:T(1,128)}, f32[2,3,64,256]{3,2,1,0:T(8,128)}, f32[2,80,256]{2,1,...) custom-call(f32[3,4,256]{2,1,0:T(4,128)} %get-tuple-element.25.refs_0_, ...), custom_call_target="tpu_custom_call" | custom-call | tf_op jit(solution)/shard_map/coupling_outputs/pallas_call | solution.py:798

commit v3 on v2

--- a/solution.py
+++ b/solution.py
@@ -16,7 +16,9 @@
 
 EDGE = 8
 BLOCK = 256
+GRAD_BLOCK = 512
 LANES = 128
+COND, RES = -1, -2
 
 
 def dot(a, b, dims=((1,), (0,)), precision=None):
@@ -32,7 +34,8 @@
 class Plan:
     def __init__(self, mesh, audio, mel, start_weight, input_weight):
         self.dp, self.tm = mesh.shape["dp"], mesh.shape["tm"]
-        self.bits = self.dp.bit_length() - 1
+        self.bits, self.tm_bits = self.dp.bit_length() - 1, self.tm.bit_length() - 1
+        self.top = self.bits + self.tm_bits - 1
         self.clips, self.group, self.frames = audio.shape
         self.half = self.group // 2
         self.cond = mel.shape[2]
@@ -45,24 +48,54 @@
         self.own_ch = self.channels // self.dp
         self.own_cond = self.cond // self.dp
         self.width = self.wide // self.tm
-        order = list(range(self.bits))
-        self.first = order
-        self.second = order[:1] + order[1:][::-1]
-        tap_pair = tuple(range(self.taps - 1))
-        rest = (self.taps - 1, "cond")
-        self.chunks = [
-            (1, tap_pair, self.wide, self.first),
-            (1, rest, self.wide, self.second),
-            (0, ("res",), self.channels, self.second),
-            (0, tap_pair, self.wide, self.first),
-            (0, rest, self.wide, self.second),
-        ]
+        near = list(range(1, self.bits))
+        far = near[::-1]
+        along = list(range(self.bits, self.bits + self.tm_bits))
+        routes = {
+            "a": [0] + near + along,
+            "b": [0] + far + along,
+            "u": [0] + near[:1] + along + near[1:],
+            "v": [0] + far[:1] + along + far[1:],
+            "z": [0] + along + near,
+            "w": [0] + along + far,
+        }
+        self.chunks = []
+        for layer, part, ways in (
+            (1, 0, "ab"),
+            (1, 1, "wu"),
+            (1, 2, "ba"),
+            (1, COND, "wb"),
+            (0, RES, "b"),
+            (0, 0, "ub"),
+            (0, 1, "ba"),
+            (0, 2, "ab"),
+            (0, COND, "bu"),
+        ):
+            high = self.part_rows(part)
+            first = high if part == RES else round_up(high // 2, 16)
+            columns = self.channels if part == RES else self.wide
+            spans = [(0, first), (first, high - first)][: len(ways)]
+            for (low, rows), way in zip(spans, ways):
+                self.chunks.append((layer, part, low, rows, columns, routes[way]))
 
     def part_rows(self, part):
-        return self.own_cond if part == "cond" else self.own_ch
-
-    def chunk_rows(self, chunk):
-        return round_up(sum(self.part_rows(part) for part in chunk[1]), 16)
+        return self.own_cond if part == COND else self.own_ch
+
+    def open_bits(self, order, stage):
+        done = set(order[: stage + 1])
+        bits = [b for b in reversed(range(self.top + 1)) if b not in done]
+        return [b for b in bits if b < self.bits], [b for b in bits if b >= self.bits]
+
+    def pieced(self, order, stage):
+        return any(b >= self.bits for b in order[: stage + 1])
+
+    def recv_shape(self, chunk, stage):
+        _, _, _, rows, columns, order = chunk
+        height = round_up(rows, 16)
+        open_dp, open_tm = self.open_bits(order, stage)
+        if self.pieced(order, stage):
+            return (2,) * len(open_tm + open_dp) + (height, self.width)
+        return (2,) * len(open_dp) + (height, columns)
 
 
 def kernel(plan, *refs):
@@ -73,12 +106,15 @@
     s = refs[n_in + n_out]
     me_dp, me_tm = lax.axis_index("dp"), lax.axis_index("tm")
     bit_of = [(me_dp // 2**b) % 2 for b in range(p.bits)]
+    bit_of += [(me_tm // 2**b) % 2 for b in range(p.tm_bits)]
     ch, rows, all_rows, fr = p.channels, p.rows, p.all_rows, p.frames
     ext = fr + 2 * EDGE
     n_blocks = ch // BLOCK
 
     def partner(b):
-        return {"dp": me_dp + (2**b) * (1 - 2 * bit_of[b]), "tm": me_tm}
+        if b < p.bits:
+            return {"dp": me_dp + (2**b) * (1 - 2 * bit_of[b]), "tm": me_tm}
+        return {"dp": me_dp, "tm": me_tm + (2 ** (b - p.bits)) * (1 - 2 * bit_of[b])}
 
     def peer(step):
         return {"dp": me_dp, "tm": lax.rem(me_tm + step, p.tm)}
@@ -94,6 +130,8 @@
         for clip in range(p.clips)
     ]
     base = 1 + p.clips
+    res_load = load(res_h, s.res, base + 2 * p.layers)
+    last_load = load(last_h, s.last, base + 2 * p.layers + 1)
     weight_loads = []
     for layer in range(p.layers):
         at = base + 2 * layer
@@ -103,15 +141,13 @@
                 load(cond_h.at[layer], s.cond.at[layer], at + 1),
             ]
         )
-        if layer == 0:
-            res_load = load(res_h, s.res, base + 2 * p.layers)
-            last_load = load(last_h, s.last, base + 2 * p.layers + 1)
 
     barrier = pltpu.get_barrier_semaphore()
     for b in range(p.bits):
         pl.semaphore_signal(barrier, 1, device_id=partner(b), device_id_type=MESH)
     for step in range(1, p.tm):
         pl.semaphore_signal(barrier, 1, device_id=peer(step), device_id_type=MESH)
+    audio_load.wait()
     pl.semaphore_wait(barrier, p.bits + p.tm - 1)
 
     has_low, has_high = me_tm > 0, me_tm < p.tm - 1
@@ -122,7 +158,7 @@
         audio_at = fr - LANES if slot == 0 else 0
         return [
             pltpu.make_async_remote_copy(
-                audio_h.at[:, :, pl.ds(audio_at, LANES)],
+                s.audio.at[:, :, pl.ds(audio_at, LANES)],
                 s.audio_halo.at[slot],
                 s.halo_send.at[slot, 0], s.halo_recv.at[slot, 0],
                 device_id=device, device_id_type=MESH,
@@ -156,126 +192,176 @@
         def _():
             to_low[index].wait_recv()
 
-    def free_bits(order, stage):
-        done = set(order[:stage])
-        return [b for b in reversed(range(p.bits)) if b not in done]
-
     def g_index(values):
-        return tuple(values[b] for b in reversed(range(p.bits)))
-
-    def g_blocks(chunk_id, stage, other):
-        order = p.chunks[chunk_id][3]
-        bit = order[stage]
-        free = free_bits(order, stage + 1)
-        for combo in itertools.product((0, 1), repeat=len(free)):
-            values = {b: bit_of[b] for b in order[:stage]}
-            values[bit] = 1 - bit_of[bit] if other else bit_of[bit]
-            values.update(zip(free, combo))
-            yield values
-
-    def recv_index(order, stage, values):
-        return tuple(values[b] for b in free_bits(order, stage + 1))
-
-    def add_block(chunk_id, stages, values):
-        order = p.chunks[chunk_id][3]
+        return tuple(values.get(b, slice(None)) for b in reversed(range(p.bits)))
+
+    def cols_of(chunk_id, values):
+        bits = p.tm_bits - 1 if narrow(chunk_id) else p.tm_bits
+        owner = sum(values[p.bits + b] * 2**b for b in range(bits))
+        return pl.ds(pl.multiple_of(owner * p.width, LANES), p.width)
+
+    def narrow(chunk_id):
+        return p.chunks[chunk_id][4] < p.wide
+
+    def when_side(chunk_id, stage, side, run):
+        if narrow(chunk_id) and p.chunks[chunk_id][5][stage] == p.top:
+            pl.when(bit_of[p.top] == side)(run)
+        else:
+            run()
+
+    def each(bits):
+        for combo in itertools.product((0, 1), repeat=len(bits)):
+            yield dict(zip(bits, combo))
+
+    def pieces(chunk_id, stage):
+        order = p.chunks[chunk_id][5]
+        if not p.pieced(order, stage):
+            return [{}]
+        open_tm = p.open_bits(order, stage)[1]
+        return [
+            combo for combo in each(open_tm)
+            if not (narrow(chunk_id) and combo.get(p.top, 0))
+        ]
+
+    def fixed_bits(chunk_id, stage):
+        order = p.chunks[chunk_id][5]
+        values = {b: bit_of[b] for b in order[:stage]}
+        values[order[stage]] = 1 - bit_of[order[stage]]
+        return values
+
+    def terms(chunk_id, stage, values, where, cols):
+        order = p.chunks[chunk_id][5]
+        for done in range(stage):
+            open_dp, open_tm = p.open_bits(order, done)
+            at = tuple(values[b] for b in open_dp) + where
+            if p.pieced(order, done):
+                at = tuple(values[b] for b in open_tm) + at
+            else:
+                at += (cols,)
+            yield s.recv[chunk_id][done][at]
+
+    def add_blocks(chunk_id, stage):
+        order = p.chunks[chunk_id][5]
         acc = s.grad[chunk_id]
-        at = g_index(values)
-        height = acc.shape[-2]
-
-        @pl.loop(0, height // 16)
-        def _(r):
-            where = (pl.ds(pl.multiple_of(r * 16, 16), 16),)
-            total = acc[at + where].astype(F32)
-            for stage in range(stages):
-                buf = s.recv[chunk_id][stage]
-                total += buf[recv_index(order, stage, values) + where].astype(F32)
-            acc[at + where] = total.astype(BF16)
-
-    def stage_copy(chunk_id, stage):
-        order = p.chunks[chunk_id][3]
-        bit = order[stage]
-        values = {b: slice(None) for b in range(p.bits)}
-        values.update({b: bit_of[b] for b in order[:stage]})
-        values[bit] = 1 - bit_of[bit]
-        return pltpu.make_async_remote_copy(
-            s.grad[chunk_id].at[g_index(values)],
-            s.recv[chunk_id][stage],
-            s.dp_send.at[chunk_id, stage], s.dp_recv.at[chunk_id, stage],
-            device_id=partner(bit), device_id_type=MESH,
-        )
-
-    def dp_send(chunk_id, stage):
+        for piece in pieces(chunk_id, stage):
+            for block in each(p.open_bits(order, stage)[0]):
+                values = {**fixed_bits(chunk_id, stage), **piece, **block}
+                split_cols = p.pieced(order, stage)
+                cols = cols_of(chunk_id, values) if split_cols else slice(None)
+
+                @pl.loop(0, acc.shape[-2] // 16)
+                def _(r, values=values, cols=cols):
+                    where = (pl.ds(pl.multiple_of(r * 16, 16), 16),)
+                    total = acc[g_index(values) + where + (cols,)].astype(F32)
+                    for term in terms(chunk_id, stage, values, where, cols):
+                        total += term.astype(F32)
+                    acc[g_index(values) + where + (cols,)] = total.astype(BF16)
+
+    def copies(chunk_id, stage):
+        order = p.chunks[chunk_id][5]
+        out = []
+        for slot, piece in enumerate(pieces(chunk_id, stage)):
+            values = {**fixed_bits(chunk_id, stage), **piece}
+            source, target = s.grad[chunk_id], s.recv[chunk_id][stage]
+            if p.pieced(order, stage):
+                source = source.at[g_index(values) + (slice(None), cols_of(chunk_id, values))]
+                if piece:
+                    target = target.at[tuple(piece.values())]
+            else:
+                source = source.at[g_index(values)]
+            out.append(
+                pltpu.make_async_remote_copy(
+                    source, target,
+                    s.grad_send.at[chunk_id, stage, slot],
+                    s.grad_recv.at[chunk_id, stage, slot],
+                    device_id=partner(order[stage]), device_id_type=MESH,
+                )
+            )
+        return out
+
+    def arrived(chunk_id, stage):
+        def run():
+            for copy in copies(chunk_id, stage):
+                copy.wait_recv()
+
+        when_side(chunk_id, stage, 0, run)
+
+    sent = [0] * len(p.chunks)
+
+    def send(chunk_id, stage):
+        if stage >= len(p.chunks[chunk_id][5]):
+            return
+        sent[chunk_id] = stage + 1
         if stage:
-            stage_copy(chunk_id, stage - 1).wait_recv()
-            for values in g_blocks(chunk_id, stage, True):
-                add_block(chunk_id, stage, values)
-        stage_copy(chunk_id, stage).start()
-
-    def owners(chunk_id):
-        return p.chunks[chunk_id][2] // p.width
-
-    def tm_copy(chunk_id, step):
-        target = lax.rem(me_tm + step, p.tm)
-        at = g_index({b: bit_of[b] for b in range(p.bits)})
-        place = lax.rem(target, owners(chunk_id))
-        cols = pl.ds(pl.multiple_of(place * p.width, LANES), p.width)
-        return pltpu.make_async_remote_copy(
-            s.grad[chunk_id].at[at + (slice(None), cols)],
-            s.tm_recv_buf[chunk_id].at[step - 1],
-            s.tm_send.at[chunk_id, step - 1], s.tm_recv.at[chunk_id, step - 1],
-            device_id={"dp": me_dp, "tm": target}, device_id_type=MESH,
-        )
-
-    def when_owner(chunk_id, position, run):
-        if owners(chunk_id) == p.tm:
-            run()
+            arrived(chunk_id, stage - 1)
+
+        def run():
+            if stage:
+                add_blocks(chunk_id, stage)
+            for copy in copies(chunk_id, stage):
+                copy.start()
+
+        when_side(chunk_id, stage, 1, run)
+
+    def result_copy(chunk_id):
+        layer, part, low, high, _, _ = p.chunks[chunk_id]
+        span = pl.ds(low, high)
+        if part == COND:
+            target = cond_o.at[layer, span]
+        elif part == RES:
+            target = res_o.at[layer, span]
         else:
-            pl.when(position < owners(chunk_id))(run)
-
-    def tm_send(chunk_id):
-        stage_copy(chunk_id, p.bits - 1).wait_recv()
-        add_block(chunk_id, p.bits, {b: bit_of[b] for b in range(p.bits)})
-        for step in range(1, p.tm):
-            when_owner(
-                chunk_id, lax.rem(me_tm + step, p.tm), tm_copy(chunk_id, step).start
-            )
+            target = in_o.at[layer, part, span]
+        return pltpu.make_async_copy(s.result[chunk_id], target, s.out_sem.at[chunk_id])
 
     def finish(chunk_id):
-        layer, parts, _, _ = p.chunks[chunk_id]
-        at = g_index({b: bit_of[b] for b in range(p.bits)})
+        _, _, _, high, _, order = p.chunks[chunk_id]
+        last = len(order) - 1
+        values = {b: bit_of[b] for b in range(p.top + 1)}
 
         def run():
-            for step in range(1, p.tm):
-                tm_copy(chunk_id, step).wait_recv()
-            cols = pl.ds(pl.multiple_of(me_tm * p.width, LANES), p.width)
-            total = s.grad[chunk_id][at + (slice(None), cols)].astype(F32)
-            for step in range(1, p.tm):
-                total += s.tm_recv_buf[chunk_id][step - 1].astype(F32)
-            row = 0
-            for part in parts:
-                high = p.part_rows(part)
-                piece = total[row : row + high]
-                if part == "cond":
-                    cond_o[layer] = piece
-                elif part == "res":
-                    res_o[layer] = piece
-                else:
-                    in_o[layer, part] = piece
-                row += high
-
-        when_owner(chunk_id, me_tm, run)
+            for copy in copies(chunk_id, last):
+                copy.wait_recv()
+            where = (pl.ds(0, high),)
+            cols = cols_of(chunk_id, values)
+            total = s.grad[chunk_id][g_index(values) + where + (cols,)].astype(F32)
+            for term in terms(chunk_id, last + 1, values, where, cols):
+                total += term.astype(F32)
+            s.result[chunk_id][...] = total
+            result_copy(chunk_id).start()
+
+        when_side(chunk_id, last, 0, run)
 
     def drain(chunk_id):
-        for stage in range(p.bits):
-            stage_copy(chunk_id, stage).wait_send()
-        for step in range(1, p.tm):
-            when_owner(
-                chunk_id, lax.rem(me_tm + step, p.tm), tm_copy(chunk_id, step).wait_send
-            )
-
+        for stage in range(len(p.chunks[chunk_id][5])):
+
+            def run(stage=stage):
+                for copy in copies(chunk_id, stage):
+                    copy.wait_send()
+
+            when_side(chunk_id, stage, 1, run)
+        when_side(
+            chunk_id, len(p.chunks[chunk_id][5]) - 1, 0, result_copy(chunk_id).wait
+        )
+
+    for clip in range(p.clips):
+        mel_loads[clip].wait()
+    s.mel_t[...] = jnp.transpose(s.mel[0:rows, :], (1, 0))
+    res_load.wait()
+    last_load.wait()
+    end_cols = end_w[...]
+    skips = [
+        dot(end_cols, s.res[:, ch:], ((1,), (1,))),
+        dot(end_cols, s.last[...], ((1,), (1,))),
+    ]
+    for layer in range(p.layers):
+        coarse = skips[layer].astype(BF16)
+        fine = skips[layer] - coarse.astype(F32)
+        s.skip_w[layer] = jnp.concatenate(
+            [coarse.astype(F32), fine], axis=0
+        ).astype(BF16)
     lane_iota = lax.broadcasted_iota(jnp.int32, (p.group, LANES), 1)
     row_iota = lax.broadcasted_iota(jnp.int32, (p.group, LANES), 0)
-    audio_load.wait()
     halo_wait(0)
     halo_lanes = p.pad_rows - rows
     blocks = [jnp.zeros((p.group, LANES), F32) for _ in range(halo_lanes // LANES)]
@@ -312,8 +398,6 @@
             first_cols[:all_rows], start8[:, cols], precision=HIGHEST
         )
 
-    for clip in range(p.clips):
-        mel_loads[clip].wait()
     halo_wait(1)
     for clip in range(p.clips):
         low = s.mel_halo[0, clip].astype(F32)[EDGE:]
@@ -353,6 +437,9 @@
 
     def block_at(start):
         return pl.ds(pl.multiple_of(start, BLOCK), BLOCK)
+
+    def grad_block_at(start):
+        return pl.ds(pl.multiple_of(start, GRAD_BLOCK), GRAD_BLOCK)
 
     def spread_state(layer):
         reach = 2**layer
@@ -391,7 +478,7 @@
             s.switch[layer, :, cols] = switch
             s.gated[layer, 0:all_rows, cols] = (tangent * switch).astype(BF16)
 
-    def gate_back(layer):
+    def gate_back(layer, taps):
         reach = 2**layer
 
         @pl.loop(0, ch // LANES)
@@ -407,7 +494,7 @@
                     lift * tangent * (1.0 - switch),
                 )
                 for side in range(2):
-                    for tap in range(p.taps):
+                    for tap in taps:
                         shift = ((tap - 1) * reach) % ext
                         moved = pltpu.roll(sides[side], shift, 0) if shift else sides[side]
                         store_extended(
@@ -415,38 +502,41 @@
                             lanes_at(tap * p.wide + side * ch + block * LANES), moved,
                         )
 
-    def put_owned(chunk_id, row, high, cols, value):
-        acc = s.grad[chunk_id]
-        for owner in range(p.dp):
-            at = tuple((owner >> b) & 1 for b in reversed(range(p.bits)))
-            acc[at + (pl.ds(row, high), cols)] = value[
-                owner * high : (owner + 1) * high
-            ].astype(BF16)
-
-    def weight_grads(chunk_id):
-        layer, parts, columns, _ = p.chunks[chunk_id]
-        row = 0
+    def ids_of(layer, part):
+        return [i for i, chunk in enumerate(p.chunks) if chunk[:2] == (layer, part)]
+
+    def weight_grads(layer, part):
+        ids = ids_of(layer, part)
+        columns = p.chunks[ids[0]][4]
+        high = p.part_rows(part)
         mid = p.taps // 2
-        for part in parts:
-            high = p.part_rows(part)
-
-            def body(n, part=part, row=row, high=high):
-                cols = block_at(n * BLOCK)
-                if part == "cond":
-                    left = s.mel_t[...]
-                    right = s.back[0:rows, block_at(mid * p.wide + n * BLOCK)]
-                elif part == "res":
-                    left = jnp.transpose(s.gated[layer, 0:rows, :], (1, 0))
-                    right = s.join[0:rows, cols]
-                else:
-                    left = s.state_t[layer]
-                    right = s.back[0:rows, block_at(part * p.wide + n * BLOCK)]
-                put_owned(chunk_id, row, high, cols, dot(left, right))
-
-            pl.loop(0, columns // BLOCK)(body)
-            row += high
-
-    def state_grad(layer, accumulate):
+
+        @pl.loop(0, columns // GRAD_BLOCK)
+        def _(n):
+            cols = grad_block_at(n * GRAD_BLOCK)
+            if part == COND:
+                left = s.mel_t[...]
+                right = s.back[0:rows, grad_block_at(mid * p.wide + n * GRAD_BLOCK)]
+            elif part == RES:
+                left = s.gated_t[...]
+                right = s.join[0:rows, cols]
+            else:
+                left = s.state_t[layer]
+                right = s.back[0:rows, grad_block_at(part * p.wide + n * GRAD_BLOCK)]
+            value = dot(left, right)
+            for owner in range(p.dp):
+                at = tuple((owner >> b) & 1 for b in reversed(range(p.bits)))
+                for chunk_id in ids:
+                    low, span = p.chunks[chunk_id][2:4]
+                    start = owner * high + low
+                    s.grad[chunk_id][at + (pl.ds(0, span), cols)] = value[
+                        start : start + span
+                    ].astype(BF16)
+
+        for chunk_id in ids:
+            send(chunk_id, 0)
+
+    def state_grad(layer, accumulate, between):
         @pl.loop(0, n_blocks)
         def _(n):
             total = None
@@ -461,14 +551,12 @@
             if accumulate:
                 total = total + s.state[:, cols]
             s.state[:, cols] = total
+            pl.when(n == 0)(between)
 
     spread_state(0)
-    s.mel_t[...] = jnp.transpose(s.mel[0:rows, :], (1, 0))
     for copy in weight_loads[0]:
         copy.wait()
     gate(0)
-    res_load.wait()
-
     @pl.loop(0, n_blocks)
     def _(n):
         cols = block_at(n * BLOCK)
@@ -477,18 +565,6 @@
         )
 
     spread_state(1)
-    last_load.wait()
-    end_cols = end_w[...]
-    skips = [
-        dot(end_cols, s.res[:, ch:], ((1,), (1,))),
-        dot(end_cols, s.last[...], ((1,), (1,))),
-    ]
-    for layer in range(p.layers):
-        coarse = skips[layer].astype(BF16)
-        fine = skips[layer] - coarse.astype(F32)
-        s.skip_w[layer] = jnp.concatenate(
-            [coarse.astype(F32), fine], axis=0
-        ).astype(BF16)
     for copy in weight_loads[1]:
         copy.wait()
     gate(1)
@@ -511,7 +587,7 @@
     grad_out = jnp.where(inside_clip, jnp.where(top, upper, lower), 0.0)
     s.scaled[...] = (jnp.where(top, latent * growth, 0.0) * scale_inv)[:, :rows]
     for clip in range(p.clips):
-        latent_o[clip] = latent[0 : p.half, clip * fr : (clip + 1) * fr]
+        s.latent[clip] = latent[0 : p.half, clip * fr : (clip + 1) * fr]
     first = s.first[...]
     head = (latent * latent)[:, :rows] * 0.5 - log_scale[:, :rows]
     loss = jnp.sum(
@@ -529,15 +605,24 @@
     ).astype(BF16)
 
     s.act[...] = dot(s.grad_cols[0:all_rows], s.skip_w[1])
-    gate_back(1)
-    weight_grads(0)
-    dp_send(0, 0)
-    weight_grads(1)
-    dp_send(1, 0)
-    dp_send(0, 1)
-    state_grad(1, False)
-    dp_send(1, 1)
-
+    gate_back(1, (1,))
+    weight_grads(1, COND)
+    weight_grads(1, 1)
+    gate_back(1, (0, 2))
+    send(6, 1)
+    weight_grads(1, 0)
+    send(2, 1)
+    send(7, 1)
+    send(3, 1)
+    weight_grads(1, 2)
+
+    def between1():
+        send(1, 1)
+        send(0, 1)
+
+    state_grad(1, False, between1)
+    send(5, 1)
+    send(4, 1)
     @pl.loop(0, ch // LANES)
     def _(block):
         cols = lanes_at(block * LANES)
@@ -545,9 +630,11 @@
             value = jnp.where(outside, 0.0, extended(s.state, clip, cols))
             store_extended(s.join, clip, cols, value)
 
-    weight_grads(2)
-    dp_send(2, 0)
-
+    s.gated_t[...] = jnp.transpose(s.gated[0, 0:rows, :], (1, 0))
+    weight_grads(0, RES)
+    send(7, 2)
+    send(3, 2)
+    send(6, 2)
     @pl.loop(0, n_blocks)
     def _(n):
         cols = block_at(n * BLOCK)
@@ -555,14 +642,38 @@
             s.join[...], s.res[cols, 0:ch], ((1,), (1,))
         ) + dot(s.grad_cols[0:all_rows], s.skip_w[0, :, cols])
 
-    gate_back(0)
-    weight_grads(3)
-    dp_send(3, 0)
-    weight_grads(4)
-    dp_send(4, 0)
-    late_stages(p, dp_send, tm_send, finish)
-    state_grad(0, True)
-
+    gate_back(0, (0, 1, 2))
+    send(8, 1)
+    send(2, 2)
+    send(1, 2)
+    send(0, 2)
+    weight_grads(0, 0)
+    send(3, 3)
+    weight_grads(0, 1)
+    send(5, 2)
+    send(4, 2)
+    weight_grads(0, COND)
+    send(10, 1)
+    send(7, 3)
+    send(9, 1)
+    weight_grads(0, 2)
+    send(12, 1)
+    send(1, 3)
+    send(11, 1)
+    send(6, 3)
+    send(8, 2)
+
+    def between0():
+        send(15, 1)
+        send(16, 1)
+        send(0, 3)
+        send(4, 3)
+        send(13, 1)
+
+    state_grad(0, True, between0)
+    send(2, 3)
+    send(14, 1)
+    send(5, 3)
     small = s.small
     lead = 2 * p.group
     start_grad = dot(first, s.state[0:rows], precision=HIGHEST)
@@ -571,6 +682,14 @@
         start_rows == p.half, jnp.broadcast_to(s.loss[0:1, 0:1], start_grad.shape),
         start_grad,
     )
+    s.small_tm[me_tm] = small[...]
+
+    def small_tm(step):
+        return pltpu.make_async_remote_copy(
+            small, s.small_tm.at[me_tm],
+            s.small_tm_send.at[step - 1], s.small_tm_recv.at[step - 1],
+            device_id=peer(step), device_id_type=MESH,
+        )
 
     def small_copy(stage):
         return pltpu.make_async_remote_copy(
@@ -579,46 +698,111 @@
             device_id=partner(stage), device_id_type=MESH,
         )
 
-    def small_tm(step):
-        return pltpu.make_async_remote_copy(
-            small, s.small_tm.at[me_tm],
-            s.small_tm_send.at[step - 1], s.small_tm_recv.at[step - 1],
-            device_id=peer(step), device_id_type=MESH,
-        )
-
     def small_step(stage):
-        small_copy(stage).wait()
-        small[...] = small[...] + s.small_recv[stage]
-
-    small_copy(0).start()
+        if stage:
+            small_copy(stage - 1).wait()
+            small[...] = small[...] + s.small_recv[stage - 1]
+        else:
+            for step in range(1, p.tm):
+                small_tm(step).wait()
+            total = s.small_tm[0]
+            for at in range(1, p.tm):
+                total += s.small_tm[at]
+            small[...] = total
+        if stage < p.bits:
+            small_copy(stage).start()
+
+    for step in range(1, p.tm):
+        small_tm(step).start()
+    send(3, 4)
+    send(9, 2)
     first_back = dot(start8[...], s.state[0:rows], ((1,), (1,)), precision=HIGHEST)
     front = first_back + first * scale_inv
     back_rows = pltpu.roll(s.scaled[...], p.half, 0)
     audio_grad = jnp.where(group_rows[:, :rows] < p.half, front, back_rows)
     for clip in range(p.clips):
-        audio_o[clip] = audio_grad[:, clip * fr : (clip + 1) * fr]
-    tail_stages(p, dp_send, tm_send, finish, small_copy, small_step, small_tm)
-
-    s.small_tm[me_tm] = small[...]
-    for step in range(1, p.tm):
-        small_tm(step).wait()
-    total = s.small_tm[0]
-    for at in range(1, p.tm):
-        total += s.small_tm[at]
+        s.audio_grad[clip] = audio_grad[:, clip * fr : (clip + 1) * fr]
+    for chunk_id, stage in (
+        (10, 2),
+        (7, 4),
+        (1, 4),
+        (0, 4),
+        (12, 2),
+        (4, 4),
+        (5, 4),
+        (11, 2),
+        (8, 3),
+    ):
+        send(chunk_id, stage)
+    small_step(0)
+    for chunk_id, stage in (
+        (9, 3),
+        (6, 4),
+        (16, 2),
+        (8, 4),
+        (15, 2),
+        (13, 2),
+        (2, 4),
+        (9, 4),
+    ):
+        send(chunk_id, stage)
+    small_step(1)
+    for chunk_id, stage in (
+        (10, 3),
+        (16, 3),
+        (11, 3),
+        (14, 2),
+        (10, 4),
+        (12, 3),
+        (15, 3),
+        (16, 4),
+    ):
+        send(chunk_id, stage)
+    small_step(2)
+    for chunk_id, stage in (
+        (13, 3),
+        (11, 4),
+        (14, 3),
+        (12, 4),
+        (15, 4),
+        (13, 4),
+        (14, 4),
+    ):
+        send(chunk_id, stage)
+    for stage in range(p.top + 1):
+        for chunk_id in range(len(p.chunks)):
+            if sent[chunk_id] == stage:
+                send(chunk_id, stage)
+    for stage in range(3, p.bits + 1):
+        small_step(stage)
+
+    total = small[...]
     m_first, m_last = total[: p.group], total[p.group : lead]
-    small_o[...] = total
     end_t = None
     for m, w in ((m_first, s.res[:, ch:]), (m_last, s.last[...])):
         for term in split(m):
             part = dot(term, w)
             end_t = part if end_t is None else end_t + part
-    end_o[...] = end_t
+    s.end_t[...] = end_t
+    others = [
+        pltpu.make_async_copy(source, target, s.out_sem.at[len(p.chunks) + at])
+        for at, (source, target) in enumerate(
+            (
+                (s.latent, latent_o), (s.audio_grad, audio_o), (small, small_o),
+                (s.end_t, end_o),
+            )
+        )
+    ]
+    for copy in others:
+        copy.start()
 
     for chunk_id in range(len(p.chunks)):
         finish(chunk_id)
 
     for chunk_id in range(len(p.chunks)):
         drain(chunk_id)
+    for copy in others:
+        copy.wait()
 
     @pl.when(has_high)
     def _():
@@ -638,59 +822,60 @@
 
 def outputs_kernel(plan, *refs):
     p = plan
-    (latent_i, audio_i, in_i, cond_i, res_i, small_i, end_i, end_w) = refs[:8]
+    held, end_w = refs[:7], refs[7]
     (
-        latent_o, audio_o, loss_o, in_o, cond_o, res_o, last_o, end_o, start_o, skip
-    ) = refs[8:]
+        latent_o, audio_o, loss_o, in_o, cond_o, res_o, last_o, end_o, start_o
+    ) = refs[8:17]
+    latent_s, audio_s, in_s, cond_s, res_s, small_s, end_s = refs[17:24]
+    skip, last_s, load_sem, store_sem = refs[24:]
     me_dp, me_tm = lax.axis_index("dp"), lax.axis_index("tm")
     lead = 2 * p.group
-    for source, target in (
-        (latent_i, latent_o), (audio_i, audio_o), (in_i, in_o), (cond_i, cond_o),
-        (end_i, end_o),
-    ):
-        target[...] = source[...]
-    loss_o[...] = small_i[lead + p.half : lead + p.half + 1, 0:1]
-    start_o[...] = small_i[lead : lead + p.half]
+    loads = [
+        pltpu.make_async_copy(source, target, load_sem.at[at])
+        for at, (source, target) in enumerate(zip(held, refs[17:24]))
+    ]
+    for at in (5, 2, 3, 4, 1, 0, 6):
+        loads[at].start()
+    stores = [
+        pltpu.make_async_copy(source, target, store_sem.at[at])
+        for at, (source, target) in enumerate(
+            (
+                (last_s, last_o), (in_s, in_o), (cond_s, cond_o), (audio_s, audio_o),
+                (latent_s, latent_o), (end_s, end_o),
+            )
+        )
+    ]
+    loads[5].wait()
     end_rows = end_w[...]
-    for at, out_ref in ((0, skip), (p.group, last_o)):
-        m_cols = jnp.transpose(small_i[at : at + p.group], (1, 0))
+
+    def spread(at, out_ref):
+        m_cols = jnp.transpose(small_s[at : at + p.group], (1, 0))
         coarse, fine = split(m_cols)
         out_ref[...] = dot(coarse, end_rows) + dot(fine, end_rows)
+
+    spread(p.group, last_s)
+    stores[0].start()
+    for load_at, store_at in ((2, 1), (3, 2), (1, 3), (0, 4), (6, 5)):
+        loads[load_at].wait()
+        stores[store_at].start()
+    loss_o[...] = small_s[lead + p.half : lead + p.half + 1, 0:1]
+    start_o[...] = small_s[lead : lead + p.half]
+    loads[4].wait()
     res_owners = p.channels // p.width
 
     @pl.when(me_tm < res_owners)
     def _():
-        res_o[...] = res_i[...]
+        res_o[...] = res_s[...]
 
     @pl.when(me_tm >= res_owners)
     def _():
+        spread(0, skip)
         cols = pl.ds(pl.multiple_of((me_tm - res_owners) * p.width, LANES), p.width)
         at = pl.ds(pl.multiple_of(me_dp * p.own_ch, p.own_ch), p.own_ch)
         res_o[0] = skip[at, cols]
 
-
-def late_stages(p, dp_send, tm_send, finish):
-    for stage in range(2, p.bits):
-        dp_send(0, stage)
-        dp_send(1, stage)
-    for chunk in (2, 3, 4):
-        dp_send(chunk, 1)
-
-
-def tail_stages(p, dp_send, tm_send, finish, small_copy, small_step, small_tm):
-    tm_send(0)
-    tm_send(1)
-    for stage in range(1, p.bits):
-        small_step(stage - 1)
-        small_copy(stage).start()
-    small_step(p.bits - 1)
-    for step in range(1, p.tm):
-        small_tm(step).start()
-    for stage in range(2, p.bits):
-        for chunk in (2, 3, 4):
-            dp_send(chunk, stage)
-    for chunk in (2, 3, 4):
-        tm_send(chunk)
+    for copy in stores:
+        copy.wait()
 
 
 def solution(mesh):
@@ -702,9 +887,6 @@
         ch, wide, dp = p.channels, p.wide, p.dp
         vmem, anywhere = pltpu.VMEM, pl.BlockSpec(memory_space=pl.ANY)
         inside = pl.BlockSpec(memory_space=pltpu.VMEM)
-        twos = (2,) * p.bits
-        heights = [p.chunk_rows(chunk) for chunk in p.chunks]
-        widths = [chunk[2] for chunk in p.chunks]
         n_chunks = len(p.chunks)
         sem = pltpu.SemaphoreType.DMA
         scratch = dict(
@@ -732,23 +914,29 @@
             skip_w=vmem((p.layers, 2 * p.group, ch), BF16),
             grad_cols=vmem((p.pad_rows, 2 * p.group), BF16),
             join=vmem((p.all_rows, ch), BF16),
+            gated_t=vmem((ch, p.rows), BF16),
             back=vmem((p.all_rows, p.taps * wide), BF16),
             small=vmem((3 * p.group, ch), F32),
             small_recv=vmem((p.bits, 3 * p.group, ch), F32),
             small_tm=vmem((p.tm, 3 * p.group, ch), F32),
-            grad=[vmem(twos + (h, w), BF16) for h, w in zip(heights, widths)],
+            grad=[
+                vmem((2,) * p.bits + p.recv_shape(chunk, 0)[-2:], BF16)
+                for chunk in p.chunks
+            ],
             recv=[
-                [vmem((2,) * (p.bits - 1 - st) + (h, w), BF16) for st in range(p.bits)]
-                for h, w in zip(heights, widths)
+                [vmem(p.recv_shape(chunk, stage), BF16) for stage in range(p.top + 1)]
+                for chunk in p.chunks
             ],
-            tm_recv_buf=[vmem((p.tm - 1, h, p.width), BF16) for h in heights],
             load_sem=sem((3 + p.clips + 2 * p.layers,)),
             halo_send=sem((2, 2)),
             halo_recv=sem((2, 2)),
-            dp_send=sem((n_chunks, p.bits)),
-            dp_recv=sem((n_chunks, p.bits)),
-            tm_send=sem((n_chunks, p.tm - 1)),
-            tm_recv=sem((n_chunks, p.tm - 1)),
+            grad_send=sem((n_chunks, p.top + 1, p.tm // 2)),
+            grad_recv=sem((n_chunks, p.top + 1, p.tm // 2)),
+            result=[vmem((chunk[3], p.width), F32) for chunk in p.chunks],
+            latent=vmem((p.clips, p.half, p.frames), F32),
+            audio_grad=vmem(audio.shape, F32),
+            end_t=vmem((p.group, ch), F32),
+            out_sem=sem((n_chunks + 4,)),
             small_send_sem=sem((p.bits,)),
             small_recv_sem=sem((p.bits,)),
             small_tm_send=sem((p.tm - 1,)),
@@ -778,7 +966,7 @@
             in_specs=[
                 anywhere, anywhere, inside, anywhere, anywhere, anywhere, anywhere, inside
             ],
-            out_specs=[inside] * 7,
+            out_specs=[anywhere] * 7,
             scratch_shapes=leaves,
             compiler_params=pltpu.CompilerParams(
                 collective_id=0, has_side_effects=True,
@@ -801,9 +989,14 @@
                 latent, audio_grad, shape((1, 1), F32), in_grad, cond_grad, res_grad,
                 shape(last_weight.shape, F32), end_grad, shape(start_weight.shape, F32),
             ],
-            in_specs=[inside] * 8,
-            out_specs=[inside] * 9,
-            scratch_shapes=[vmem((ch, ch), F32)],
+            in_specs=[anywhere] * 7 + [inside],
+            out_specs=[
+                anywhere, anywhere, inside, anywhere, anywhere, inside, anywhere, anywhere,
+                inside,
+            ],
+            scratch_shapes=[vmem(leaf.shape, F32) for leaf in held]
+            + [vmem((ch, ch), F32)] * 2
+            + [sem((7,)), sem((6,))],
             name="coupling_outputs",
         )(*held, end_t)
         outs = list(outs)

time: 96.4 us -> 79.4 us (0.82)
  Pallas kernels: 95.5 us -> 78.2 us
    pallas_call x1, Pallas kernels: 92.4 us -> 74.3 us  [shards(): pl.pallas_call(entry, out_shape=[latent, audio_grad, in_grad, cond_grad,...]
where the time goes in v3:
time: 79.4 us; the launch traced here: 79 us
  Pallas kernels  78.2 us (98%)
  between operations  0.81 us (1%)
    pallas_call x1, Pallas kernels, shards(): pl.pallas_call(entry, out_shape=[latent, audio_grad, in_grad, cond_grad,...  74.3 us
    pallas_call x1, Pallas kernels, shards(): pl.pallas_call(lambda *refs: outputs_kernel(p, *refs), out_shape=[latent,...  3.87 us

profile of v3, /device:TPU:0, one launch (start us, length us, event | category | flops | bytes accessed | tf_op | source)
XLA Modules:
  0.0 79.0 jit_solution(13164960504220935028)
XLA Ops:
  0.6 74.3 %coupling_step.1 = (f32[3,4,256]{2,1,0:T(4,128)}, f32[3,8,256]{2,1,0:T(8,128)}, f32[2,3,64,256]{3,2,1,0:T(8,128)}, f32[2,80,256]{2,1,0:T(8,128)}, f32[1,64,256]{...) custom-call(f32[3,8,256]{2,1,0:T(8,128)} %refs_0_.1, bf16[3,256,640]{2,1,0:T(8,128)(2,1)} %refs_1_.1, ...), custom_call_target="tpu_custom_call" | custom-call | tf_op jit(solution)/shard_map/coupling_step/pallas_call | solution.py:960
  75.0 3.9 %coupling_outputs.1 = (f32[3,4,256]{2,1,0:T(4,128)}, f32[3,8,256]{2,1,0:T(8,128)}, f32[1,1]{1,0:T(1,128)}, f32[2,3,64,256]{3,2,1,0:T(8,128)}, f32[2,80,256]{2,1,...) custom-call(f32[3,4,256]{2,1,0:T(4,128)} %get-tuple-element.25.refs_0_, ...), custom_call_target="tpu_custom_call" | custom-call | tf_op jit(solution)/shard_map/coupling_outputs/pallas_call | solution.py:986

commit v4 on v3

--- a/solution.py
+++ b/solution.py
@@ -260,6 +260,7 @@
     def copies(chunk_id, stage):
         order = p.chunks[chunk_id][5]
         out = []
+        before = sum(2 ** len(p.open_bits(order, k)[1]) if p.pieced(order, k) else 1 for k in range(stage))
         for slot, piece in enumerate(pieces(chunk_id, stage)):
             values = {**fixed_bits(chunk_id, stage), **piece}
             source, target = s.grad[chunk_id], s.recv[chunk_id][stage]
@@ -272,8 +273,8 @@
             out.append(
                 pltpu.make_async_remote_copy(
                     source, target,
-                    s.grad_send.at[chunk_id, stage, slot],
-                    s.grad_recv.at[chunk_id, stage, slot],
+                    s.grad_send.at[chunk_id, slot],
+                    s.grad_recv.at[chunk_id, before + slot],
                     device_id=partner(order[stage]), device_id_type=MESH,
                 )
             )
@@ -285,6 +286,13 @@
                 copy.wait_recv()
 
         when_side(chunk_id, stage, 0, run)
+
+    def left(chunk_id, stage):
+        def run():
+            for copy in copies(chunk_id, stage):
+                copy.wait_send()
+
+        when_side(chunk_id, stage, 1, run)
 
     sent = [0] * len(p.chunks)
 
@@ -294,6 +302,7 @@
         sent[chunk_id] = stage + 1
         if stage:
             arrived(chunk_id, stage - 1)
+            left(chunk_id, stage - 1)
 
         def run():
             if stage:
@@ -333,13 +342,7 @@
         when_side(chunk_id, last, 0, run)
 
     def drain(chunk_id):
-        for stage in range(len(p.chunks[chunk_id][5])):
-
-            def run(stage=stage):
-                for copy in copies(chunk_id, stage):
-                    copy.wait_send()
-
-            when_side(chunk_id, stage, 1, run)
+        left(chunk_id, len(p.chunks[chunk_id][5]) - 1)
         when_side(
             chunk_id, len(p.chunks[chunk_id][5]) - 1, 0, result_copy(chunk_id).wait
         )
@@ -822,50 +825,32 @@
 
 def outputs_kernel(plan, *refs):
     p = plan
-    held, end_w = refs[:7], refs[7]
+    (latent_i, audio_i, in_i, cond_i, res_i, small_i, end_i, end_w) = refs[:8]
     (
-        latent_o, audio_o, loss_o, in_o, cond_o, res_o, last_o, end_o, start_o
-    ) = refs[8:17]
-    latent_s, audio_s, in_s, cond_s, res_s, small_s, end_s = refs[17:24]
-    skip, last_s, load_sem, store_sem = refs[24:]
+        latent_o, audio_o, loss_o, in_o, cond_o, res_o, last_o, end_o, start_o, skip
+    ) = refs[8:]
     me_dp, me_tm = lax.axis_index("dp"), lax.axis_index("tm")
     lead = 2 * p.group
-    loads = [
-        pltpu.make_async_copy(source, target, load_sem.at[at])
-        for at, (source, target) in enumerate(zip(held, refs[17:24]))
-    ]
-    for at in (5, 2, 3, 4, 1, 0, 6):
-        loads[at].start()
-    stores = [
-        pltpu.make_async_copy(source, target, store_sem.at[at])
-        for at, (source, target) in enumerate(
-            (
-                (last_s, last_o), (in_s, in_o), (cond_s, cond_o), (audio_s, audio_o),
-                (latent_s, latent_o), (end_s, end_o),
-            )
-        )
-    ]
-    loads[5].wait()
+    for source, target in (
+        (latent_i, latent_o), (audio_i, audio_o), (in_i, in_o), (cond_i, cond_o),
+        (end_i, end_o),
+    ):
+        target[...] = source[...]
+    loss_o[...] = small_i[lead + p.half : lead + p.half + 1, 0:1]
+    start_o[...] = small_i[lead : lead + p.half]
     end_rows = end_w[...]
 
     def spread(at, out_ref):
-        m_cols = jnp.transpose(small_s[at : at + p.group], (1, 0))
+        m_cols = jnp.transpose(small_i[at : at + p.group], (1, 0))
         coarse, fine = split(m_cols)
         out_ref[...] = dot(coarse, end_rows) + dot(fine, end_rows)
 
-    spread(p.group, last_s)
-    stores[0].start()
-    for load_at, store_at in ((2, 1), (3, 2), (1, 3), (0, 4), (6, 5)):
-        loads[load_at].wait()
-        stores[store_at].start()
-    loss_o[...] = small_s[lead + p.half : lead + p.half + 1, 0:1]
-    start_o[...] = small_s[lead : lead + p.half]
-    loads[4].wait()
+    spread(p.group, last_o)
     res_owners = p.channels // p.width
 
     @pl.when(me_tm < res_owners)
     def _():
-        res_o[...] = res_s[...]
+        res_o[...] = res_i[...]
 
     @pl.when(me_tm >= res_owners)
     def _():
@@ -873,9 +858,6 @@
         cols = pl.ds(pl.multiple_of((me_tm - res_owners) * p.width, LANES), p.width)
         at = pl.ds(pl.multiple_of(me_dp * p.own_ch, p.own_ch), p.own_ch)
         res_o[0] = skip[at, cols]
-
-    for copy in stores:
-        copy.wait()
 
 
 def solution(mesh):
@@ -930,8 +912,8 @@
             load_sem=sem((3 + p.clips + 2 * p.layers,)),
             halo_send=sem((2, 2)),
             halo_recv=sem((2, 2)),
-            grad_send=sem((n_chunks, p.top + 1, p.tm // 2)),
-            grad_recv=sem((n_chunks, p.top + 1, p.tm // 2)),
+            grad_send=sem((n_chunks, p.tm // 2)),
+            grad_recv=sem((n_chunks, p.bits + p.tm - 1)),
             result=[vmem((chunk[3], p.width), F32) for chunk in p.chunks],
             latent=vmem((p.clips, p.half, p.frames), F32),
             audio_grad=vmem(audio.shape, F32),
@@ -989,14 +971,9 @@
                 latent, audio_grad, shape((1, 1), F32), in_grad, cond_grad, res_grad,
                 shape(last_weight.shape, F32), end_grad, shape(start_weight.shape, F32),
             ],
-            in_specs=[anywhere] * 7 + [inside],
-            out_specs=[
-                anywhere, anywhere, inside, anywhere, anywhere, inside, anywhere, anywhere,
-                inside,
-            ],
-            scratch_shapes=[vmem(leaf.shape, F32) for leaf in held]
-            + [vmem((ch, ch), F32)] * 2
-            + [sem((7,)), sem((6,))],
+            in_specs=[inside] * 8,
+            out_specs=[inside] * 9,
+            scratch_shapes=[vmem((ch, ch), F32)],
             name="coupling_outputs",
         )(*held, end_t)
         outs = list(outs)

time: 79.4 us -> 76.3 us (0.961)
  Pallas kernels: 78.2 us -> 75.4 us
    pallas_call x1, Pallas kernels: 74.3 us -> 72.5 us  [shards(): pl.pallas_call(entry, out_shape=[latent, audio_grad, in_grad, cond_grad,...]
    pallas_call x1, Pallas kernels: 3.87 us -> 2.86 us  [shards(): pl.pallas_call(lambda *refs: outputs_kernel(p, *refs), out_shape=[latent,...]
where the time goes in v4:
time: 76.3 us; the launch traced here: 76.1 us
  Pallas kernels  75.4 us (99%)
    pallas_call x1, Pallas kernels, shards(): pl.pallas_call(entry, out_shape=[latent, audio_grad, in_grad, cond_grad,...  72.5 us
    pallas_call x1, Pallas kernels, shards(): pl.pallas_call(lambda *refs: outputs_kernel(p, *refs), out_shape=[latent,...  2.86 us

profile of v4, /device:TPU:0, one launch (start us, length us, event | category | flops | bytes accessed | tf_op | source)
XLA Modules:
  0.0 76.1 jit_solution(1794990099506499933)
XLA Ops:
  0.6 72.5 %coupling_step.1 = (f32[3,4,256]{2,1,0:T(4,128)}, f32[3,8,256]{2,1,0:T(8,128)}, f32[2,3,64,256]{3,2,1,0:T(8,128)}, f32[2,80,256]{2,1,0:T(8,128)}, f32[1,64,256]{...) custom-call(f32[3,8,256]{2,1,0:T(8,128)} %refs_0_.1, bf16[3,256,640]{2,1,0:T(8,128)(2,1)} %refs_1_.1, ...), custom_call_target="tpu_custom_call" | custom-call | tf_op jit(solution)/shard_map/coupling_step/pallas_call | solution.py:942
  73.2 2.9 %coupling_outputs.1 = (f32[3,4,256]{2,1,0:T(4,128)}, f32[3,8,256]{2,1,0:T(8,128)}, f32[1,1]{1,0:T(1,128)}, f32[2,3,64,256]{3,2,1,0:T(8,128)}, f32[2,80,256]{2,1,...) custom-call(f32[3,4,256]{2,1,0:T(4,128)} %get-tuple-element.25.refs_0_, ...), custom_call_target="tpu_custom_call" | custom-call | tf_op jit(solution)/shard_map/coupling_outputs/pallas_call | solution.py:968
